TPU v7x, 256 devices: a whole 4x4x8 slice. The times are simulated.
256 devices in a mesh: ctx: 32 (over z, y), head: 8 (over x, core).
Axes of the slice: x: 4, y: 4, z: 8, core: 2. Of those that a mesh axis runs over, the one named last changes fastest.
Arguments:
- query_input: bfloat16 [16384, 4096], P(('ctx', 'head')), may hold values from -6 to 6
- key_input: bfloat16 [16384, 4096], P(('ctx', 'head')), may hold values from -6 to 6
- value_input: bfloat16 [16384, 4096], P(('ctx', 'head')), may hold values from -6 to 6
- cotangent: bfloat16 [16384, 4096], P(('ctx', 'head')), may hold values from -6 to 6
- level_codes: int32 [32, 15, 16384], P('head', None, 'ctx'), may hold values from 0 to 15
Outputs:
- attended: bfloat16 [16384, 4096], P(('ctx', 'head'))
- grad_queries: bfloat16 [16384, 4096], P(('ctx', 'head'))
- grad_keys: bfloat16 [16384, 4096], P(('ctx', 'head'))
- grad_values: bfloat16 [16384, 4096], P(('ctx', 'head'))
All inputs are finite; a program needn't handle non-finite values.
Results may differ from a plain program's by a relative error of at most 0.0074.
Values may be sent and summed in bfloat16 or wider, within the bound.
A program may use at most 128 MiB of HBM per device.

v0:
```python
import jax
import jax.numpy as jnp
from jax import lax
from jax.sharding import PartitionSpec as P


def swapped(block, axis, stride):
    count = lax.axis_size(axis)
    route = []
    for low in range(count):
        high = low | 1 << stride
        if high != low and high < count:
            route += [(low, high), (high, low)]
    return lax.ppermute(block, axis, route)


def for_sending(x):

    def short(part):
        return part.astype(jnp.bfloat16) if part.dtype == jnp.float32 else part

    return jax.tree.map(short, x)


def level_gain(level):
    if level == 0:
        return 1.0
    return 2.0 ** (-(level - 1) / 2.0)


def on_device(query_input, key_input, value_input, cotangent, level_codes):
    query_rows, key_rows, value_rows, cot_rows = (
        lax.all_to_all(query_input, "head", split_axis=1, concat_axis=0, tiled=True),
        lax.all_to_all(key_input, "head", split_axis=1, concat_axis=0, tiled=True),
        lax.all_to_all(value_input, "head", split_axis=1, concat_axis=0, tiled=True),
        lax.all_to_all(cotangent, "head", split_axis=1, concat_axis=0, tiled=True),
    )
    head_count = level_codes.shape[0]
    total_levels = level_codes.shape[1]
    length = query_rows.shape[0]
    head_dim = query_rows.shape[1] // head_count
    tok_bits = length.bit_length() - 1
    ctx_bits = total_levels - tok_bits - 1
    score_scale = head_dim ** (-0.5)
    head_shape = (length, head_count, head_dim)
    query_heads = query_rows.reshape(head_shape)
    key_heads = key_rows.reshape(head_shape)
    value_heads = value_rows.reshape(head_shape)
    cot_heads = cot_rows.reshape(head_shape)
    code_weights = level_codes.astype(jnp.float32) / 8.0
    my_block = lax.axis_index("ctx")
    cross_scale = jnp.stack(
        [
            code_weights[:, tok_bits + 1 + bit_index, :]
            * (score_scale * level_gain(tok_bits + 1 + bit_index))
            * (my_block // 2**bit_index % 2).astype(jnp.float32)
            for bit_index in range(ctx_bits)
        ]
    )
    row_scale = jnp.transpose(cross_scale, (0, 2, 1))
    block_state = jnp.einsum(
        "phd,phe->hde", key_heads, value_heads, preferred_element_type=jnp.float32
    )
    scaled_cot = (row_scale[..., None] * cot_heads[None]).astype(jnp.bfloat16)
    grad_state = jnp.einsum(
        "phd,bphe->bhde", query_heads, scaled_cot, preferred_element_type=jnp.float32
    )
    running = block_state
    bucket_list = []
    for bit_index in range(ctx_bits):
        partner = swapped(running.astype(jnp.bfloat16), "ctx", bit_index).astype(running.dtype)
        bit_set = (my_block // 2**bit_index % 2).astype(jnp.float32)
        bucket_list.append(bit_set * partner)
        running = running + partner
    bucket_sums = jnp.stack(bucket_list)
    bucket = bucket_sums.astype(jnp.bfloat16)
    carried = [grad_state[level_index] for level_index in range(ctx_bits)]
    pulled = jnp.zeros((head_count, head_dim, head_dim), jnp.float32)
    for bit_index in range(ctx_bits):
        partner = swapped(for_sending(jnp.stack(carried)), "ctx", bit_index)
        bit_clear = 1.0 - (my_block // 2**bit_index % 2).astype(jnp.float32)
        pulled = pulled + bit_clear * partner[0]
        carried = [
            carried[level_index + 1] + partner[level_index + 1]
            for level_index in range(len(carried) - 1)
        ]
    pulled_half = pulled.astype(jnp.bfloat16)
    block_rows = min(512, length)
    steps_count = length // block_rows
    places = jnp.arange(length, dtype=jnp.int32)

    def row_step(carried_grads, block_index):
        key_grad, value_grad = carried_grads
        first_row = block_index * block_rows
        rows_at = first_row + jnp.arange(block_rows, dtype=jnp.int32)
        levels = jnp.zeros((block_rows, length), jnp.int32)
        for bit_index in range(tok_bits):
            levels = levels + (
                rows_at[:, None] // 2**bit_index != places[None, :] // 2**bit_index
            ).astype(jnp.int32)
        weight = jnp.zeros((head_count, block_rows, length), jnp.float32)
        for level_index in range(tok_bits + 1):
            weight = jnp.where(
                (levels == level_index)[None],
                code_weights[:, level_index, :, None] * level_gain(level_index),
                weight,
            )
        weight = jnp.where((places[None, :] <= rows_at[:, None])[None], weight, 0.0)
        scores = jnp.einsum(
            "phd,shd->hps", query_heads, key_heads, preferred_element_type=jnp.float32
        )
        attention = (score_scale * weight * scores).astype(jnp.bfloat16)
        local_out = jnp.einsum(
            "hps,she->phe", attention, value_heads, preferred_element_type=jnp.float32
        )
        dots = jnp.einsum(
            "phe,she->hps", cot_heads, value_heads, preferred_element_type=jnp.float32
        )
        score_grads = (score_scale * weight * dots).astype(jnp.bfloat16)
        local_qgrad = jnp.einsum(
            "hps,shd->phd", score_grads, key_heads, preferred_element_type=jnp.float32
        )
        key_grad = key_grad + jnp.einsum(
            "hps,phd->shd", score_grads, query_heads, preferred_element_type=jnp.float32
        )
        value_grad = value_grad + jnp.einsum(
            "hps,phe->she", attention, cot_heads, preferred_element_type=jnp.float32
        )
        return ((key_grad, value_grad), (local_out, local_qgrad))

    zero_grads = jnp.zeros(head_shape, jnp.float32)
    (key_local, value_local), (local_out, local_qgrad) = lax.scan(
        row_step, (zero_grads, zero_grads), jnp.arange(steps_count, dtype=jnp.int32)
    )
    local_out = local_out.reshape(head_shape)
    local_qgrad = local_qgrad.reshape(head_shape)
    cross_out = jnp.sum(
        row_scale[..., None]
        * jnp.einsum("phd,bhde->bphe", query_heads, bucket, preferred_element_type=jnp.float32),
        axis=0,
    )
    cross_qgrad = jnp.sum(
        row_scale[..., None]
        * jnp.einsum("phe,bhde->bphd", cot_heads, bucket, preferred_element_type=jnp.float32),
        axis=0,
    )
    flat_shape = (length, head_count * head_dim)
    attended = (local_out + cross_out).astype(jnp.bfloat16).reshape(flat_shape)
    grad_query = (local_qgrad + cross_qgrad).astype(jnp.bfloat16).reshape(flat_shape)
    grad_key = (
        (
            key_local
            + jnp.einsum(
                "phe,hde->phd", value_heads, pulled_half, preferred_element_type=jnp.float32
            )
        )
        .astype(jnp.bfloat16)
        .reshape(flat_shape)
    )
    grad_value = (
        (
            value_local
            + jnp.einsum("phd,hde->phe", key_heads, pulled_half, preferred_element_type=jnp.float32)
        )
        .astype(jnp.bfloat16)
        .reshape(flat_shape)
    )
    return (
        lax.all_to_all(attended, "head", split_axis=0, concat_axis=1, tiled=True),
        lax.all_to_all(grad_query, "head", split_axis=0, concat_axis=1, tiled=True),
        lax.all_to_all(grad_key, "head", split_axis=0, concat_axis=1, tiled=True),
        lax.all_to_all(grad_value, "head", split_axis=0, concat_axis=1, tiled=True),
    )


def solution(mesh):
    return jax.shard_map(
        on_device,
        mesh=mesh,
        in_specs=(
            P(("ctx", "head"), None),
            P(("ctx", "head"), None),
            P(("ctx", "head"), None),
            P(("ctx", "head"), None),
            P("head", None, "ctx"),
        ),
        out_specs=(
            P(("ctx", "head"), None),
            P(("ctx", "head"), None),
            P(("ctx", "head"), None),
            P(("ctx", "head"), None),
        ),
        check_vma=False,
    )
```

profile of v0, /device:TPU:1, one launch (start us, length us, event | category | flops | bytes accessed | tf_op | source)
XLA Modules:
  0.0 212.4 jit_solution(3397119964379641207)
XLA Ops:
  0.7 1.9 copy.194
  2.6 6.7 %all-to-all-start.2 = ((bf16[64,8,512]{2,0,1:T(8,128)(2,1)}), bf16[64,8,512]{2,0,1:T(8,128)(2,1)S(1)}, u32[]{:S(2)}, u32[]{:S(2)}) async-start(bf16[64,8,512]{2,0,1:T(8,128)(2,1)} %bitcast.140), calls=%async_computation.2 | async-start | bytes 1048576 | tf_op jit(solution)/shard_map/all_to_all | solution.py:35
  9.5 0.8 copy.195
  10.4 8.3 %all-to-all-done.2 = bf16[64,8,512]{2,0,1:T(8,128)(2,1)S(1)} async-done(((bf16[64,8,512]{2,0,1:T(8,128)(2,1)}), bf16[64,8,512]{2,0,1:T(8,128)(2,1)S(1)}, u32[]{:S(2)}, u32[]{:S(2)}) %all-to-all-start.2) | async-done | bytes 524320 | tf_op jit(solution)/shard_map/all_to_all | solution.py:35
  18.7 4.4 %all-to-all-start.1 = ((bf16[64,8,512]{2,0,1:T(8,128)(2,1)}), bf16[64,8,512]{2,0,1:T(8,128)(2,1)S(1)}, u32[]{:S(2)}, u32[]{:S(2)}) async-start(bf16[64,8,512]{2,0,1:T(8,128)(2,1)} %bitcast.141), calls=%async_computation.1 | async-start | bytes 1048576 | tf_op jit(solution)/shard_map/all_to_all | solution.py:34
  23.7 0.8 copy.196
  24.6 0.8 copy.193
  25.5 6.9 %all-to-all-done.1 = bf16[64,8,512]{2,0,1:T(8,128)(2,1)S(1)} async-done(((bf16[64,8,512]{2,0,1:T(8,128)(2,1)}), bf16[64,8,512]{2,0,1:T(8,128)(2,1)S(1)}, u32[]{:S(2)}, u32[]{:S(2)}) %all-to-all-start.1) | async-done | bytes 524320 | tf_op jit(solution)/shard_map/all_to_all | solution.py:34
  32.5 4.4 %all-to-all-start = ((bf16[64,8,512]{2,0,1:T(8,128)(2,1)}), bf16[64,8,512]{2,0,1:T(8,128)(2,1)S(1)}, u32[]{:S(2)}, u32[]{:S(2)}) async-start(bf16[64,8,512]{2,0,1:T(8,128)(2,1)} %bitcast.142), calls=%async_computation | async-start | bytes 1048576 | tf_op jit(solution)/shard_map/all_to_all | solution.py:33
  36.8 3.9 %broadcast_compare_fusion.9 = (pred[512,512]{1,0:T(8,128)(4,1)}, pred[512,512]{1,0:T(8,128)(4,1)}, pred[512,512]{1,0:T(8,128)(4,1)}, pred[512,512]{1,0:T(8,128)(...) fusion(s32[512]{0:T(512)S(1)} %get-tuple-element.70, ...), kind=kLoop, calls=%fused_computation.46 | loop fusion | flops 9437184 | bytes 2637824 | tf_op jit(solution)/shard_map/while/body/eval_jaxpr/eq | solution.py:104
  40.8 5.4 %all-to-all-done = bf16[64,8,512]{2,0,1:T(8,128)(2,1)S(1)} async-done(((bf16[64,8,512]{2,0,1:T(8,128)(2,1)}), bf16[64,8,512]{2,0,1:T(8,128)(2,1)S(1)}, u32[]{:S(2)}, u32[]{:S(2)}) %all-to-all-start) | async-done | bytes 524320 | tf_op jit(solution)/shard_map/all_to_all | solution.py:33
  46.2 4.4 %all-to-all-start.4 = ((bf16[64,8,512]{2,0,1:T(8,128)(2,1)}), bf16[64,8,512]{2,0,1:T(8,128)(2,1)S(1)}, u32[]{:S(2)}, u32[]{:S(2)}) async-start(bf16[64,8,512]{2,0,1:T(8,128)(2,1)} %bitcast.139), calls=%async_computation.4 | async-start | bytes 1048576 | tf_op jit(solution)/shard_map/all_to_all | solution.py:36
  50.9 1.0 fusion.89
  52.4 0.9 reshape.3029
  53.3 6.6 %all-to-all-done.4 = bf16[64,8,512]{2,0,1:T(8,128)(2,1)S(1)} async-done(((bf16[64,8,512]{2,0,1:T(8,128)(2,1)}), bf16[64,8,512]{2,0,1:T(8,128)(2,1)S(1)}, u32[]{:S(2)}, u32[]{:S(2)}) %all-to-all-start.4) | async-done | bytes 524320 | tf_op jit(solution)/shard_map/all_to_all | solution.py:36
  60.1 1.3 copy.112
  61.6 7.4 %multiply_convert_fusion.1 = bf16[4,512,512]{2,1,0:T(8,128)(2,1)} fusion(f32[4,512]{1,0:T(4,128)S(1)} %get-tuple-element.47, f32[4,512]{1,0:T(4,128)S(1)} %get-tuple-element.48, f32[4,512]{1,0:T(4,128)S(1)} %get-tuple-element.49, f32[4,512]{1,0:T(4,128)S(1)} %get-tuple-element.50, f32[4,512]{1,0:T(4,128)S(1)} %get-tuple-element.51, ...), kind=kOutput, calls=%fused_computation.5 | convolution fusion | flops 283115520 | bytes 6111232 | tf_op jit(solution)/shard_map/while/body/eval_jaxpr/phe,she->hps/dot_general | solution.py:116
  69.1 6.4 %multiply_convert_fusion.2 = bf16[4,512,512]{2,1,0:T(8,128)(2,1)S(1)} fusion(f32[4,512]{1,0:T(4,128)S(1)} %get-tuple-element.47, f32[4,512]{1,0:T(4,128)} %copy-done.25, f32[4,512]{1,0:T(4,128)} %copy-done.26, f32[4,512]{1,0:T(4,128)} %copy-done.27, f32[4,512]{1,0:T(4,128)} %copy-done.28, f32[4,512]{1,0:T(4,128)} %copy-done.29, f32[4,512]{1,0:T(4,128)} %copy-done.30, ...), kind=kOutput, calls=%fused_computation.6 | convolution fusion | flops 283115520 | bytes 6111232 | tf_op jit(solution)/shard_map/while/body/eval_jaxpr/phd,shd->hps/dot_general | solution.py:109
  75.5 0.9 fusion.90
  77.0 2.7 %collective-permute-start.1 = (bf16[4,128,128]{2,1,0:T(8,128)(2,1)S(1)}, bf16[4,128,128]{2,1,0:T(8,128)(2,1)S(1)}, u32[]{:S(2)}, u32[]{:S(2)}) collective-permute-start(bf16[4,128,128]{2,1,0:T(8,128)(2,1)S(1)} %fusion.40), channel_id=1, source_target_pairs={{0,16},{16,0},{8,24},{24,8},{32,48},{48,32},{40,56},{56,40},{64,80... | collective-permute-start | bytes 393224 | tf_op jit(solution)/shard_map/ppermute | solution.py:14
  79.7 16.2 %collective-permute-done.1 = bf16[4,128,128]{2,1,0:T(8,128)(2,1)S(1)} collective-permute-done((bf16[4,128,128]{2,1,0:T(8,128)(2,1)S(1)}, bf16[4,128,128]{2,1,0:T(8,128)(2,1)S(1)}, u32[]{:S(2)}, u32[]{:S(2)}) %collective-permute-start.1) | collective-permute-done | bytes 131104 | tf_op jit(solution)/shard_map/ppermute | solution.py:14
  96.0 1.7 collective-permute-start.2
  97.8 2.3 %collective-permute-done.2 = bf16[4,128,128]{2,1,0:T(8,128)(2,1)S(1)} collective-permute-done((bf16[4,128,128]{2,1,0:T(8,128)(2,1)S(1)}, bf16[4,128,128]{2,1,0:T(8,128)(2,1)S(1)}, u32[]{:S(2)}, u32[]{:S(2)}) %collective-permute-start.2) | collective-permute-done | bytes 131104 | tf_op jit(solution)/shard_map/ppermute | solution.py:14
  100.2 3.1 %collective-permute-start.3 = (bf16[4,128,128]{2,1,0:T(8,128)(2,1)S(1)}, bf16[4,128,128]{2,1,0:T(8,128)(2,1)S(1)}, u32[]{:S(2)}, u32[]{:S(2)}) collective-permute-start(bf16[4,128,128]{2,1,0:T(8,128)(2,1)S(1)} %fusion.41), channel_id=1, source_target_pairs={{0,64},{64,0},{8,72},{72,8},{16,80},{80,16},{24,88},{88,24},{32,96... | collective-permute-start | bytes 393224 | tf_op jit(solution)/shard_map/ppermute | solution.py:14
  103.3 3.7 %collective-permute-done.3 = bf16[4,128,128]{2,1,0:T(8,128)(2,1)S(1)} collective-permute-done((bf16[4,128,128]{2,1,0:T(8,128)(2,1)S(1)}, bf16[4,128,128]{2,1,0:T(8,128)(2,1)S(1)}, u32[]{:S(2)}, u32[]{:S(2)}) %collective-permute-start.3) | collective-permute-done | bytes 131104 | tf_op jit(solution)/shard_map/ppermute | solution.py:14
  107.1 6.2 %collective-permute-start.4 = (bf16[4,128,128]{2,1,0:T(8,128)(2,1)S(1)}, bf16[4,128,128]{2,1,0:T(8,128)(2,1)S(1)}, u32[]{:S(2)}, u32[]{:S(2)}) collective-permute-start(bf16[4,128,128]{2,1,0:T(8,128)(2,1)S(1)} %fusion.36), channel_id=1, source_target_pairs={{0,128},{128,0},{8,136},{136,8},{16,144},{144,16},{24,152},{152,24... | collective-permute-start | bytes 393224 | tf_op jit(solution)/shard_map/ppermute | solution.py:14
  114.2 0.9 pad_maximum_fusion
  115.8 0.8 copy-done.24
  116.7 1.9 fusion.1
  118.6 2.5 %copy.98 = f32[512,4,128]{2,0,1:T(8,128)} copy(f32[512,4,128]{0,2,1:T(8,128)} %fusion.1) | data formatting | bytes 2097152 | tf_op jit(solution)/shard_map/reduce_sum | solution.py:137
  121.2 4.5 %collective-permute-done.6 = bf16[4,4,128,128]{2,3,0,1:T(8,128)(2,1)} collective-permute-done((bf16[4,4,128,128]{2,3,0,1:T(8,128)(2,1)}, bf16[4,4,128,128]{2,3,0,1:T(8,128)(2,1)}, u32[]{:S(2)}, u32[]{:S(2)}) %collective-permute-start.6) | collective-permute-done | bytes 524320 | tf_op jit(solution)/shard_map/ppermute | solution.py:14
  125.6 1.5 add_convert_fusion.3
  127.1 0.9 pad_maximum_fusion.1
  128.7 1.2 copy.99
  129.9 2.0 convert_element_type.688
  131.9 9.6 %all-to-all-start.3 = ((bf16[8,64,512]{2,1,0:T(8,128)(2,1)}), bf16[8,64,512]{2,1,0:T(8,128)(2,1)}, u32[]{:S(2)}, u32[]{:S(2)}) async-start(bf16[8,64,512]{2,1,0:T(8,128)(2,1)} %convert_element_type.688), calls=%async_computation.3 | async-start | bytes 1048576 | tf_op jit(solution)/shard_map/all_to_all | solution.py:169
  141.6 3.2 %fusion = f32[512,4,128]{0,2,1:T(8,128)} fusion(f32[5,512,4]{1,0,2:T(8,128)} %copy.93, bf16[5,4,128,128]{3,2,1,0:T(8,128)(2,1)} %copy-done.24, bf16[512,4,128,1]{2,1,0,3:T(4,128)(2,1)} %bitcast.143), kind=kOutput, calls=%fused_computation.1 | convolution fusion | flops 337903616 | bytes 2269184 | tf_op jit(solution)/shard_map/phe,bhde->bphd/dot_general | solution.py:144
  144.8 2.5 %copy.107 = f32[512,4,128]{2,0,1:T(8,128)} copy(f32[512,4,128]{0,2,1:T(8,128)} %fusion) | data formatting | bytes 2097152 | tf_op jit(solution)/shard_map/reduce_sum | solution.py:142
  147.3 1.6 add_convert_fusion.2
  149.6 3.1 %collective-permute-start.8 = (bf16[2,4,128,128]{2,3,0,1:T(8,128)(2,1)}, bf16[2,4,128,128]{2,3,0,1:T(8,128)(2,1)}, u32[]{:S(2)}, u32[]{:S(2)}) collective-permute-start(bf16[2,4,128,128]{2,3,0,1:T(8,128)(2,1)} %pad_maximum_fusion.2), channel_id=1, source_target_pairs={{0,64},{64,0},{8,72},{72,8},{16,80},{80,16},{24,88},{88,24},{32,96... | collective-permute-start | bytes 786440 | tf_op jit(solution)/shard_map/ppermute | solution.py:14
  152.7 2.0 fusion.10
  154.7 1.2 copy.108
  155.9 2.0 convert_element_type.691
  157.9 7.3 %collective-permute-done.8 = bf16[2,4,128,128]{2,3,0,1:T(8,128)(2,1)} collective-permute-done((bf16[2,4,128,128]{2,3,0,1:T(8,128)(2,1)}, bf16[2,4,128,128]{2,3,0,1:T(8,128)(2,1)}, u32[]{:S(2)}, u32[]{:S(2)}) %collective-permute-start.8) | collective-permute-done | bytes 262176 | tf_op jit(solution)/shard_map/ppermute | solution.py:14
  165.2 1.9 add_convert_fusion.1
  167.1 1.4 collective-permute-start.9
  168.5 5.4 %all-to-all-start.5 = ((bf16[8,64,512]{2,1,0:T(8,128)(2,1)}), bf16[8,64,512]{2,1,0:T(8,128)(2,1)}, u32[]{:S(2)}, u32[]{:S(2)}) async-start(bf16[8,64,512]{2,1,0:T(8,128)(2,1)} %convert_element_type.691), calls=%async_computation.5 | async-start | bytes 1048576 | tf_op jit(solution)/shard_map/all_to_all | solution.py:170
  173.9 2.6 %convolution_bitcast_fusion.1 = f32[512,4,128]{2,0,1:T(8,128)S(1)} fusion(bf16[4,512,512]{2,1,0:T(8,128)(2,1)} %multiply_convert_fusion.1, bf16[512,4,128]{2,1,0:T(4,128)(2,1)} %reshape.3029), kind=kOutput, calls=%fused_computation.13 | convolution fusion | flops 268435456 | bytes 3670016 | tf_op jit(solution)/shard_map/while/body/eval_jaxpr/hps,phd->shd/dot_general | solution.py:123
  176.4 1.4 collective-permute-done.9
  177.8 1.5 fusion.13
  179.3 1.2 copy.117
  180.5 2.0 all_to_all.118
  182.5 0.8 all-to-all-done.5
  183.3 5.0 %all-to-all-start.6 = ((bf16[8,64,512]{2,1,0:T(8,128)(2,1)}), bf16[8,64,512]{2,1,0:T(8,128)(2,1)}, u32[]{:S(2)}, u32[]{:S(2)}) async-start(bf16[8,64,512]{2,1,0:T(8,128)(2,1)} %all_to_all.118), calls=%async_computation.6 | async-start | bytes 1048576 | tf_op jit(solution)/shard_map/all_to_all | solution.py:171
  188.3 0.9 convolution_bitcast_fusion
  189.2 1.5 fusion.12
  191.1 1.0 all_to_all.122
  192.1 5.7 %all-to-all-done.6 = bf16[8,64,512]{2,1,0:T(8,128)(2,1)} async-done(((bf16[8,64,512]{2,1,0:T(8,128)(2,1)}), bf16[8,64,512]{2,1,0:T(8,128)(2,1)}, u32[]{:S(2)}, u32[]{:S(2)}) %all-to-all-start.6) | async-done | bytes 524320 | tf_op jit(solution)/shard_map/all_to_all | solution.py:171
  197.8 4.4 %all-to-all-start.7 = ((bf16[8,64,512]{2,1,0:T(8,128)(2,1)}), bf16[8,64,512]{2,1,0:T(8,128)(2,1)S(1)}, u32[]{:S(2)}, u32[]{:S(2)}) async-start(bf16[8,64,512]{2,1,0:T(8,128)(2,1)} %all_to_all.122), calls=%async_computation.7 | async-start | bytes 1048576 | tf_op jit(solution)/shard_map/all_to_all | solution.py:172
  202.2 1.9 copy.145
  204.1 1.9 copy.146
  205.9 1.9 copy.147
  207.8 3.7 %all-to-all-done.7 = bf16[8,64,512]{2,1,0:T(8,128)(2,1)S(1)} async-done(((bf16[8,64,512]{2,1,0:T(8,128)(2,1)}), bf16[8,64,512]{2,1,0:T(8,128)(2,1)S(1)}, u32[]{:S(2)}, u32[]{:S(2)}) %all-to-all-start.7) | async-done | bytes 524320 | tf_op jit(solution)/shard_map/all_to_all | solution.py:172
  211.6 0.8 copy.148
  (103 shorter events, 6.3 us)
Async XLA Ops:
  0.6 8.7 %copy-start.22 = (s32[4,15,512]{2,0,1:T(4,128)S(1)}, s32[4,15,512]{2,0,1:T(4,128)}, u32[]{:S(2)}) copy-start(s32[4,15,512]{2,0,1:T(4,128)} %param.9) | copy-start | bytes 368644
  0.6 8.9 %copy-start.8 = (bf16[64,4096]{1,0:T(8,128)(2,1)S(1)}, bf16[64,4096]{1,0:T(8,128)(2,1)}, u32[]{:S(2)}) copy-start(bf16[64,4096]{1,0:T(8,128)(2,1)} %param.6) | copy-start | bytes 1572868
  2.6 21.1 %copy-start.9 = (bf16[64,4096]{1,0:T(8,128)(2,1)S(1)}, bf16[64,4096]{1,0:T(8,128)(2,1)}, u32[]{:S(2)}) copy-start(bf16[64,4096]{1,0:T(8,128)(2,1)} %param.5) | copy-start | bytes 1572868
  2.6 16.1 %all-to-all-start.2 = ((bf16[64,8,512]{2,0,1:T(8,128)(2,1)}), bf16[64,8,512]{2,0,1:T(8,128)(2,1)S(1)}, u32[]{:S(2)}, u32[]{:S(2)}) async-start(bf16[64,8,512]{2,0,1:T(8,128)(2,1)} %bitcast.140), calls=%async_computation.2 | async-start | bytes 1048576 | tf_op jit(solution)/shard_map/all_to_all | solution.py:35
  9.3 15.2 %copy-start.10 = (bf16[64,4096]{1,0:T(8,128)(2,1)S(1)}, bf16[64,4096]{1,0:T(8,128)(2,1)}, u32[]{:S(2)}) copy-start(bf16[64,4096]{1,0:T(8,128)(2,1)} %param.8) | copy-start | bytes 1572868
  18.7 13.7 %all-to-all-start.1 = ((bf16[64,8,512]{2,0,1:T(8,128)(2,1)}), bf16[64,8,512]{2,0,1:T(8,128)(2,1)S(1)}, u32[]{:S(2)}, u32[]{:S(2)}) async-start(bf16[64,8,512]{2,0,1:T(8,128)(2,1)} %bitcast.141), calls=%async_computation.1 | async-start | bytes 1048576 | tf_op jit(solution)/shard_map/all_to_all | solution.py:34
  25.5 35.9 %copy-start.11 = (pred[512,512]{1,0:T(8,128)(4,1)}, pred[512,512]{1,0:T(8,128)(4,1)S(1)}, u32[]{:S(2)}) copy-start(pred[512,512]{1,0:T(8,128)(4,1)S(1)} %iota_compare_fusion.1) | copy-start | bytes 786436
  32.5 13.7 %all-to-all-start = ((bf16[64,8,512]{2,0,1:T(8,128)(2,1)}), bf16[64,8,512]{2,0,1:T(8,128)(2,1)S(1)}, u32[]{:S(2)}, u32[]{:S(2)}) async-start(bf16[64,8,512]{2,0,1:T(8,128)(2,1)} %bitcast.142), calls=%async_computation | async-start | bytes 1048576 | tf_op jit(solution)/shard_map/all_to_all | solution.py:33
  46.2 13.7 %all-to-all-start.4 = ((bf16[64,8,512]{2,0,1:T(8,128)(2,1)}), bf16[64,8,512]{2,0,1:T(8,128)(2,1)S(1)}, u32[]{:S(2)}, u32[]{:S(2)}) async-start(bf16[64,8,512]{2,0,1:T(8,128)(2,1)} %bitcast.139), calls=%async_computation.4 | async-start | bytes 1048576 | tf_op jit(solution)/shard_map/all_to_all | solution.py:36
  50.6 10.8 %copy-start.25 = (f32[4,512]{1,0:T(4,128)}, f32[4,512]{1,0:T(4,128)S(1)}, u32[]{:S(2)}) copy-start(f32[4,512]{1,0:T(4,128)S(1)} %get-tuple-element.48) | copy-start | bytes 24580
  50.6 10.8 %copy-start.26 = (f32[4,512]{1,0:T(4,128)}, f32[4,512]{1,0:T(4,128)S(1)}, u32[]{:S(2)}) copy-start(f32[4,512]{1,0:T(4,128)S(1)} %get-tuple-element.49) | copy-start | bytes 24580
  50.6 10.8 %copy-start.27 = (f32[4,512]{1,0:T(4,128)}, f32[4,512]{1,0:T(4,128)S(1)}, u32[]{:S(2)}) copy-start(f32[4,512]{1,0:T(4,128)S(1)} %get-tuple-element.50) | copy-start | bytes 24580
  50.6 10.8 %copy-start.28 = (f32[4,512]{1,0:T(4,128)}, f32[4,512]{1,0:T(4,128)S(1)}, u32[]{:S(2)}) copy-start(f32[4,512]{1,0:T(4,128)S(1)} %get-tuple-element.51) | copy-start | bytes 24580
  50.6 10.8 %copy-start.29 = (f32[4,512]{1,0:T(4,128)}, f32[4,512]{1,0:T(4,128)S(1)}, u32[]{:S(2)}) copy-start(f32[4,512]{1,0:T(4,128)S(1)} %get-tuple-element.52) | copy-start | bytes 24580
  50.6 10.8 %copy-start.30 = (f32[4,512]{1,0:T(4,128)}, f32[4,512]{1,0:T(4,128)S(1)}, u32[]{:S(2)}) copy-start(f32[4,512]{1,0:T(4,128)S(1)} %get-tuple-element.53) | copy-start | bytes 24580
  50.6 10.8 %copy-start.31 = (f32[4,512]{1,0:T(4,128)}, f32[4,512]{1,0:T(4,128)S(1)}, u32[]{:S(2)}) copy-start(f32[4,512]{1,0:T(4,128)S(1)} %get-tuple-element.54) | copy-start | bytes 24580
  50.6 10.8 %copy-start.32 = (f32[4,512]{1,0:T(4,128)}, f32[4,512]{1,0:T(4,128)S(1)}, u32[]{:S(2)}) copy-start(f32[4,512]{1,0:T(4,128)S(1)} %get-tuple-element.55) | copy-start | bytes 24580
  51.9 25.0 %collective-permute-start = (bf16[4,128,128]{2,1,0:T(8,128)(2,1)}, bf16[4,128,128]{2,1,0:T(8,128)(2,1)S(1)}, u32[]{:S(2)}, u32[]{:S(2)}) collective-permute-start(bf16[4,128,128]{2,1,0:T(8,128)(2,1)} %get-tuple-element.66), channel_id=1, source_target_pairs={{0,8},{8,0},{16,24},{24,16},{32,40},{40,32},{48,56},{56,48},{64,72... | collective-permute-start | bytes 393224 | tf_op jit(solution)/shard_map/ppermute | solution.py:14
  60.1 1.4 copy-start.2
  61.5 7.5 %copy-start.6 = (bf16[512,4,128]{2,1,0:T(4,128)(2,1)S(1)}, bf16[512,4,128]{2,1,0:T(4,128)(2,1)}, u32[]{:S(2)}) copy-start(bf16[512,4,128]{2,1,0:T(4,128)(2,1)} %reshape.3029) | copy-start | bytes 1572868
  61.5 7.5 %copy-start.12 = (pred[512,512]{1,0:T(8,128)(4,1)S(1)}, pred[512,512]{1,0:T(8,128)(4,1)}, u32[]{:S(2)}) copy-start(pred[512,512]{1,0:T(8,128)(4,1)} %get-tuple-element.56) | copy-start | bytes 786436
  61.5 7.5 %copy-start.13 = (pred[512,512]{1,0:T(8,128)(4,1)S(1)}, pred[512,512]{1,0:T(8,128)(4,1)}, u32[]{:S(2)}) copy-start(pred[512,512]{1,0:T(8,128)(4,1)} %get-tuple-element.57) | copy-start | bytes 786436
  61.5 7.5 %copy-start.14 = (pred[512,512]{1,0:T(8,128)(4,1)S(1)}, pred[512,512]{1,0:T(8,128)(4,1)}, u32[]{:S(2)}) copy-start(pred[512,512]{1,0:T(8,128)(4,1)} %get-tuple-element.58) | copy-start | bytes 786436
  61.5 7.5 %copy-start.15 = (pred[512,512]{1,0:T(8,128)(4,1)S(1)}, pred[512,512]{1,0:T(8,128)(4,1)}, u32[]{:S(2)}) copy-start(pred[512,512]{1,0:T(8,128)(4,1)} %get-tuple-element.59) | copy-start | bytes 786436
  61.5 7.5 %copy-start.16 = (pred[512,512]{1,0:T(8,128)(4,1)S(1)}, pred[512,512]{1,0:T(8,128)(4,1)}, u32[]{:S(2)}) copy-start(pred[512,512]{1,0:T(8,128)(4,1)} %get-tuple-element.60) | copy-start | bytes 786436
  61.5 7.5 %copy-start.17 = (pred[512,512]{1,0:T(8,128)(4,1)S(1)}, pred[512,512]{1,0:T(8,128)(4,1)}, u32[]{:S(2)}) copy-start(pred[512,512]{1,0:T(8,128)(4,1)} %get-tuple-element.61) | copy-start | bytes 786436
  61.5 7.5 %copy-start.18 = (pred[512,512]{1,0:T(8,128)(4,1)S(1)}, pred[512,512]{1,0:T(8,128)(4,1)}, u32[]{:S(2)}) copy-start(pred[512,512]{1,0:T(8,128)(4,1)} %get-tuple-element.62) | copy-start | bytes 786436
  61.5 7.5 %copy-start.19 = (pred[512,512]{1,0:T(8,128)(4,1)S(1)}, pred[512,512]{1,0:T(8,128)(4,1)}, u32[]{:S(2)}) copy-start(pred[512,512]{1,0:T(8,128)(4,1)} %get-tuple-element.63) | copy-start | bytes 786436
  61.6 7.5 %copy-start.20 = (pred[512,512]{1,0:T(8,128)(4,1)S(1)}, pred[512,512]{1,0:T(8,128)(4,1)}, u32[]{:S(2)}) copy-start(pred[512,512]{1,0:T(8,128)(4,1)} %get-tuple-element.64) | copy-start | bytes 786436
  61.6 7.5 %copy-start.21 = (pred[512,512]{1,0:T(8,128)(4,1)S(1)}, pred[512,512]{1,0:T(8,128)(4,1)}, u32[]{:S(2)}) copy-start(pred[512,512]{1,0:T(8,128)(4,1)} %get-tuple-element.65) | copy-start | bytes 786436
  69.1 6.4 %copy-start.7 = (f32[512,4,128]{0,2,1:T(8,128)S(1)}, f32[512,4,128]{0,2,1:T(8,128)}, u32[]{:S(2)}) copy-start(f32[512,4,128]{0,2,1:T(8,128)} %copy.112) | copy-start | bytes 3145732
  69.1 6.4 %copy-start.23 = (f32[5,512,4]{1,0,2:T(8,128)S(1)}, f32[5,512,4]{1,0,2:T(8,128)}, u32[]{:S(2)}) copy-start(f32[5,512,4]{1,0,2:T(8,128)} %copy.93) | copy-start | bytes 122884
  76.4 37.1 %copy-start.1 = (f32[5,4,128,128]{2,3,0,1:T(8,128)}, f32[5,4,128,128]{2,3,0,1:T(8,128)S(1)}, u32[]{:S(2)}) copy-start(f32[5,4,128,128]{2,3,0,1:T(8,128)S(1)} %get-tuple-element.69) | copy-start | bytes 3932164
  76.4 36.9 %collective-permute-start.5 = (bf16[5,4,128,128]{2,3,0,1:T(8,128)(2,1)S(1)}, bf16[5,4,128,128]{2,3,0,1:T(8,128)(2,1)S(1)}, u32[]{:S(2)}, u32[]{:S(2)}) collective-permute-start(bf16[5,4,128,128]{2,3,0,1:T(8,128)(2,1)S(1)} %get-tuple-element.68), channel_id=1, source_target_pairs={{0,8},{8,0},{16,24},{24,16},{32,40},{40,32},{48,56},{56,48},{64,72... | collective-permute-start | bytes 1966088 | tf_op jit(solution)/shard_map/ppermute | solution.py:14
  77.0 19.0 %collective-permute-start.1 = (bf16[4,128,128]{2,1,0:T(8,128)(2,1)S(1)}, bf16[4,128,128]{2,1,0:T(8,128)(2,1)S(1)}, u32[]{:S(2)}, u32[]{:S(2)}) collective-permute-start(bf16[4,128,128]{2,1,0:T(8,128)(2,1)S(1)} %fusion.40), channel_id=1, source_target_pairs={{0,16},{16,0},{8,24},{24,8},{32,48},{48,32},{40,56},{56,40},{64,80... | collective-permute-start | bytes 393224 | tf_op jit(solution)/shard_map/ppermute | solution.py:14
  96.0 4.1 %collective-permute-start.2 = (bf16[4,128,128]{2,1,0:T(8,128)(2,1)S(1)}, bf16[4,128,128]{2,1,0:T(8,128)(2,1)S(1)}, u32[]{:S(2)}, u32[]{:S(2)}) collective-permute-start(bf16[4,128,128]{2,1,0:T(8,128)(2,1)S(1)} %fusion.87), channel_id=1, source_target_pairs={{0,32},{32,0},{8,40},{40,8},{16,48},{48,16},{24,56},{56,24},{64,96... | collective-permute-start | bytes 393224 | tf_op jit(solution)/shard_map/ppermute | solution.py:14
  100.2 6.8 %collective-permute-start.3 = (bf16[4,128,128]{2,1,0:T(8,128)(2,1)S(1)}, bf16[4,128,128]{2,1,0:T(8,128)(2,1)S(1)}, u32[]{:S(2)}, u32[]{:S(2)}) collective-permute-start(bf16[4,128,128]{2,1,0:T(8,128)(2,1)S(1)} %fusion.41), channel_id=1, source_target_pairs={{0,64},{64,0},{8,72},{72,8},{16,80},{80,16},{24,88},{88,24},{32,96... | collective-permute-start | bytes 393224 | tf_op jit(solution)/shard_map/ppermute | solution.py:14
  107.1 8.7 %collective-permute-start.4 = (bf16[4,128,128]{2,1,0:T(8,128)(2,1)S(1)}, bf16[4,128,128]{2,1,0:T(8,128)(2,1)S(1)}, u32[]{:S(2)}, u32[]{:S(2)}) collective-permute-start(bf16[4,128,128]{2,1,0:T(8,128)(2,1)S(1)} %fusion.36), channel_id=1, source_target_pairs={{0,128},{128,0},{8,136},{136,8},{16,144},{144,16},{24,152},{152,24... | collective-permute-start | bytes 393224 | tf_op jit(solution)/shard_map/ppermute | solution.py:14
  113.3 0.9 copy-start.5
  115.0 10.6 %collective-permute-start.6 = (bf16[4,4,128,128]{2,3,0,1:T(8,128)(2,1)}, bf16[4,4,128,128]{2,3,0,1:T(8,128)(2,1)}, u32[]{:S(2)}, u32[]{:S(2)}) collective-permute-start(bf16[4,4,128,128]{2,3,0,1:T(8,128)(2,1)} %pad_maximum_fusion), channel_id=1, source_target_pairs={{0,16},{16,0},{8,24},{24,8},{32,48},{48,32},{40,56},{56,40},{64,80... | collective-permute-start | bytes 1572872 | tf_op jit(solution)/shard_map/ppermute | solution.py:14
  115.8 0.8 copy-start.24
  121.1 6.8 %copy-start.4 = (f32[512,4,128]{2,0,1:T(8,128)S(1)}, f32[512,4,128]{2,0,1:T(8,128)}, u32[]{:S(2)}) copy-start(f32[512,4,128]{2,0,1:T(8,128)} %copy.98) | copy-start | bytes 3145732
  128.0 19.4 %collective-permute-start.7 = (bf16[3,4,128,128]{2,3,0,1:T(8,128)(2,1)}, bf16[3,4,128,128]{2,3,0,1:T(8,128)(2,1)S(1)}, u32[]{:S(2)}, u32[]{:S(2)}) collective-permute-start(bf16[3,4,128,128]{2,3,0,1:T(8,128)(2,1)} %pad_maximum_fusion.1), channel_id=1, source_target_pairs={{0,32},{32,0},{8,40},{40,8},{16,48},{48,16},{24,56},{56,24},{64,96... | collective-permute-start | bytes 1179656 | tf_op jit(solution)/shard_map/ppermute | solution.py:14
  131.9 36.5 %all-to-all-start.3 = ((bf16[8,64,512]{2,1,0:T(8,128)(2,1)}), bf16[8,64,512]{2,1,0:T(8,128)(2,1)}, u32[]{:S(2)}, u32[]{:S(2)}) async-start(bf16[8,64,512]{2,1,0:T(8,128)(2,1)} %convert_element_type.688), calls=%async_computation.3 | async-start | bytes 1048576 | tf_op jit(solution)/shard_map/all_to_all | solution.py:169
  147.3 5.4 %copy-start = (bf16[4,512,512]{2,1,0:T(8,128)(2,1)S(1)}, bf16[4,512,512]{2,1,0:T(8,128)(2,1)}, u32[]{:S(2)}) copy-start(bf16[4,512,512]{2,1,0:T(8,128)(2,1)} %multiply_convert_fusion.1) | copy-start | bytes 6291460
  149.6 15.6 %collective-permute-start.8 = (bf16[2,4,128,128]{2,3,0,1:T(8,128)(2,1)}, bf16[2,4,128,128]{2,3,0,1:T(8,128)(2,1)}, u32[]{:S(2)}, u32[]{:S(2)}) collective-permute-start(bf16[2,4,128,128]{2,3,0,1:T(8,128)(2,1)} %pad_maximum_fusion.2), channel_id=1, source_target_pairs={{0,64},{64,0},{8,72},{72,8},{16,80},{80,16},{24,88},{88,24},{32,96... | collective-permute-start | bytes 786440 | tf_op jit(solution)/shard_map/ppermute | solution.py:14
  167.1 10.7 %collective-permute-start.9 = (bf16[1,4,128,128]{2,3,0,1:T(8,128)(2,1)}, bf16[1,4,128,128]{2,3,0,1:T(8,128)(2,1)}, u32[]{:S(2)}, u32[]{:S(2)}) collective-permute-start(bf16[1,4,128,128]{2,3,0,1:T(8,128)(2,1)} %add_convert_fusion.1), channel_id=1, source_target_pairs={{0,128},{128,0},{8,136},{136,8},{16,144},{144,16},{24,152},{152,24... | collective-permute-start | bytes 393224 | tf_op jit(solution)/shard_map/ppermute | solution.py:14
  168.5 14.9 %all-to-all-start.5 = ((bf16[8,64,512]{2,1,0:T(8,128)(2,1)}), bf16[8,64,512]{2,1,0:T(8,128)(2,1)}, u32[]{:S(2)}, u32[]{:S(2)}) async-start(bf16[8,64,512]{2,1,0:T(8,128)(2,1)} %convert_element_type.691), calls=%async_computation.5 | async-start | bytes 1048576 | tf_op jit(solution)/shard_map/all_to_all | solution.py:170
  179.3 9.1 %copy-start.3 = (bf16[512,4,128]{2,1,0:T(4,128)(2,1)S(1)}, bf16[512,4,128]{2,1,0:T(4,128)(2,1)}, u32[]{:S(2)}) copy-start(bf16[512,4,128]{2,1,0:T(4,128)(2,1)} %copy-done.2) | copy-start | bytes 1572868
  183.3 14.5 %all-to-all-start.6 = ((bf16[8,64,512]{2,1,0:T(8,128)(2,1)}), bf16[8,64,512]{2,1,0:T(8,128)(2,1)}, u32[]{:S(2)}, u32[]{:S(2)}) async-start(bf16[8,64,512]{2,1,0:T(8,128)(2,1)} %all_to_all.118), calls=%async_computation.6 | async-start | bytes 1048576 | tf_op jit(solution)/shard_map/all_to_all | solution.py:171
  197.8 13.7 %all-to-all-start.7 = ((bf16[8,64,512]{2,1,0:T(8,128)(2,1)}), bf16[8,64,512]{2,1,0:T(8,128)(2,1)S(1)}, u32[]{:S(2)}, u32[]{:S(2)}) async-start(bf16[8,64,512]{2,1,0:T(8,128)(2,1)} %all_to_all.122), calls=%async_computation.7 | async-start | bytes 1048576 | tf_op jit(solution)/shard_map/all_to_all | solution.py:172
where the time goes:
time: 214 us; the launch traced here: 212 us
  waiting for transfers between devices  73.3 us (34%)
  starting transfers between devices  63.8 us (30%)
  local copies, waits for them, and re-layouts  32.1 us (15%)
  matrix products  29.9 us (14%)
  other arithmetic  12.1 us (6%)
    ppermute x10, waiting for transfers between devices, swapped(): return lax.ppermute(block, axis, route)  35.7 us
    ppermute x10, starting transfers between devices, swapped(): return lax.ppermute(block, axis, route)  19.5 us
    all_to_all x1, starting transfers between devices, on_device(): lax.all_to_all(attended, 'head', split_axis=0, concat_axis=1, tiled=True)  9.64 us
    all_to_all x1, waiting for transfers between devices, on_device(): lax.all_to_all(value_input, 'head', split_axis=1, concat_axis=0, tiled=True)  8.33 us
    dot_general x1, matrix products, row_step(): jnp.einsum('phe,she->hps', cot_heads, value_heads, preferred_element_type...  7.41 us
    all_to_all x1, waiting for transfers between devices, on_device(): lax.all_to_all(key_input, 'head', split_axis=1, concat_axis=0, tiled=True)  6.93 us
    all_to_all x1, starting transfers between devices, on_device(): lax.all_to_all(value_input, 'head', split_axis=1, concat_axis=0, tiled=True)  6.73 us
    all_to_all x1, waiting for transfers between devices, on_device(): lax.all_to_all(cotangent, 'head', split_axis=1, concat_axis=0, tiled=True)  6.63 us
  transfers between devices with their start and end apart: 18, of which 14 were waited for; matrix products, arithmetic and copies ran while one was open for 30% of the time, Pallas kernels for 0%

commit v1 on v0

v1 whole, which is shorter than its diff:
```python
import functools

import jax
import jax.numpy as jnp
from jax import lax
from jax.experimental import pallas as pl
from jax.experimental.pallas import tpu as pltpu
from jax.sharding import PartitionSpec as P

MESH = pl.DeviceIdType.MESH
KEY, VALUE, QUERY, COT = range(4)
TILE = 128


def level_gain(level):
    if level == 0:
        return 1.0
    return 2.0 ** (-(level - 1) / 2.0)


def dot_nn(a, b):
    return lax.dot_general(a, b, (((1,), (0,)), ((), ())), preferred_element_type=jnp.float32)


def dot_nt(a, b):
    return lax.dot_general(a, b, (((1,), (1,)), ((), ())), preferred_element_type=jnp.float32)


def dot_tn(a, b):
    return lax.dot_general(a, b, (((0,), (0,)), ((), ())), preferred_element_type=jnp.float32)


def kernel(
    n_ctx,
    n_head,
    ctx_bits,
    tok_bits,
    query_ref,
    key_ref,
    value_ref,
    cot_ref,
    codes_ref,
    out_ref,
    gq_ref,
    gk_ref,
    gv_ref,
    rows_in,
    codes,
    code_rows,
    code_cols,
    levels,
    local,
    rows_out,
    state_send,
    state_parts,
    bucket_send,
    bucket,
    grad_send,
    grad_parts,
    pulled_send,
    pulled,
    in_send,
    in_recv,
    own_sem,
    state_sems,
    bucket_send_sem,
    bucket_recv,
    grad_send_sem,
    grad_recv,
    pulled_sems,
    out_send,
    out_recv,
):
    my_ctx = lax.axis_index("ctx")
    my_head = lax.axis_index("head")
    inputs = (key_ref, value_ref, query_ref, cot_ref)
    outputs = (out_ref, gq_ref, gk_ref, gv_ref)
    share = query_ref.shape[0]
    length = share * n_head
    width = query_ref.shape[1] // n_head
    n_local = width // TILE
    state_rows = n_local * TILE
    part = state_rows // n_ctx
    tiles = length // TILE
    scale = TILE ** (-0.5)

    def bit_set(block, bit_index):
        return block // 2**bit_index % 2 == 1

    def own_bit(bit_index):
        return bit_set(my_ctx, bit_index)

    def ctx_peer(step):
        return lax.rem(my_ctx + step, n_ctx)

    def head_columns(head):
        return pl.ds(pl.multiple_of(head * TILE, TILE), TILE)

    def part_rows(owner):
        return pl.ds(pl.multiple_of(owner * part, part), part)

    def share_rows(owner):
        return pl.ds(pl.multiple_of(owner * share, share), share)

    def width_columns(owner):
        return pl.ds(pl.multiple_of(owner * width, width), width)

    barrier = pltpu.get_barrier_semaphore()
    for step in range(1, n_head):
        pl.semaphore_signal(
            barrier, inc=1, device_id={"head": lax.rem(my_head + step, n_head)}, device_id_type=MESH
        )

    @pl.loop(1, n_ctx)
    def _(step):
        pl.semaphore_signal(barrier, inc=1, device_id={"ctx": ctx_peer(step)}, device_id_type=MESH)

    codes_copy = pltpu.make_async_copy(codes_ref, codes, own_sem.at[8])
    codes_copy.start()
    for slot, array in enumerate(inputs):
        pltpu.make_async_copy(
            array.at[:, width_columns(my_head)],
            rows_in.at[slot, share_rows(my_head), :],
            own_sem.at[slot],
        ).start()
    pl.semaphore_wait(barrier, n_head - 1 + n_ctx - 1)

    for slot, array in enumerate(inputs):
        for step in range(1, n_head):
            peer = lax.rem(my_head + step, n_head)
            pltpu.make_async_remote_copy(
                src_ref=array.at[:, width_columns(peer)],
                dst_ref=rows_in.at[slot, share_rows(my_head), :],
                send_sem=in_send.at[slot],
                recv_sem=in_recv.at[slot],
                device_id={"head": peer},
                device_id_type=MESH,
            ).start()

    codes_copy.wait()
    for head in range(n_local):
        code_rows[...] = jnp.zeros_like(code_rows)
        code_rows[0 : codes.shape[1], :] = codes[head].astype(jnp.float32)
        code_cols[head] = code_rows[...].T
    place = lax.broadcasted_iota(jnp.int32, (TILE, TILE), 0)
    other = lax.broadcasted_iota(jnp.int32, (TILE, TILE), 1)
    differ = place ^ other
    level = jnp.zeros((TILE, TILE), jnp.int32)
    for bit_index in range(7):
        level = level + (differ >= 2**bit_index).astype(jnp.int32)
    levels[...] = jnp.where(other <= place, level, -1)
    for bit_index in range(ctx_bits):

        @pl.when(jnp.logical_not(own_bit(bit_index)))
        def _():
            bucket[bit_index] = jnp.zeros((state_rows, TILE), jnp.bfloat16)

    def arrived(slot):
        pltpu.make_async_copy(
            inputs[slot].at[:, width_columns(my_head)],
            rows_in.at[slot, share_rows(my_head), :],
            own_sem.at[slot],
        ).wait()
        others = rows_in.at[slot, 0 : length - share, :]
        pltpu.make_async_copy(others, others, in_recv.at[slot]).wait()

    def code_column(head, level_index, rows):
        return code_cols[head, rows, level_index : level_index + 1] * (
            level_gain(level_index) * scale / 8.0
        )

    arrived(KEY)
    arrived(VALUE)

    @pl.loop(0, n_local)
    def _(head):
        columns = head_columns(head)
        state = dot_tn(rows_in[KEY, :, columns], rows_in[VALUE, :, columns])
        state_send[columns, :] = state.astype(jnp.bfloat16)

    @pl.loop(1, n_ctx)
    def _(step):
        peer = ctx_peer(step)
        pltpu.make_async_remote_copy(
            src_ref=state_send.at[part_rows(peer), :],
            dst_ref=state_parts.at[my_ctx],
            send_sem=state_sems.at[0],
            recv_sem=state_sems.at[1],
            device_id={"ctx": peer},
            device_id_type=MESH,
        ).start()

    state_parts[my_ctx] = state_send[part_rows(my_ctx), :]
    state_others = state_parts.at[0 : n_ctx - 1]
    pltpu.make_async_copy(state_others, state_others, state_sems.at[1]).wait()

    node = state_parts[...].astype(jnp.float32)
    first_node = []
    count = 0
    for bit_index in range(ctx_bits):
        pairs = node.reshape(node.shape[0] // 2, 2, part, TILE)
        first_node.append(count)
        bucket_send[count : count + pairs.shape[0]] = pairs[:, 0].astype(jnp.bfloat16)
        count += pairs.shape[0]
        node = pairs[:, 0] + pairs[:, 1]

    @pl.loop(1, n_ctx)
    def _(step):
        peer = ctx_peer(step)
        for bit_index in range(ctx_bits):

            @pl.when(bit_set(peer, bit_index))
            def _():
                pltpu.make_async_remote_copy(
                    src_ref=bucket_send.at[first_node[bit_index] + peer // 2 ** (bit_index + 1)],
                    dst_ref=bucket.at[bit_index, part_rows(my_ctx), :],
                    send_sem=bucket_send_sem.at[bit_index],
                    recv_sem=bucket_recv.at[bit_index],
                    device_id={"ctx": peer},
                    device_id_type=MESH,
                ).start()

    for bit_index in range(ctx_bits):

        @pl.when(own_bit(bit_index))
        def _():
            bucket[bit_index, part_rows(my_ctx), :] = bucket_send[
                first_node[bit_index] + my_ctx // 2 ** (bit_index + 1)
            ]

    arrived(QUERY)
    arrived(COT)

    @pl.loop(0, n_local)
    def _(head):
        columns = head_columns(head)
        query = rows_in[QUERY, :, columns]
        cot = rows_in[COT, :, columns].astype(jnp.float32)
        for bit_index in range(ctx_bits):
            row_scale = code_column(head, tok_bits + 1 + bit_index, slice(None))
            scaled = (row_scale * cot).astype(jnp.bfloat16)
            grad_send[bit_index, columns, :] = dot_tn(query, scaled).astype(jnp.bfloat16)

    def grad_slot(block, bit_index):
        return block // 2 ** (bit_index + 1) * 2**bit_index + block % 2**bit_index

    @pl.loop(1, n_ctx)
    def _(step):
        peer = ctx_peer(step)
        for bit_index in range(ctx_bits):

            @pl.when(own_bit(bit_index))
            def _():
                pltpu.make_async_remote_copy(
                    src_ref=grad_send.at[bit_index, part_rows(peer), :],
                    dst_ref=grad_parts.at[bit_index, grad_slot(my_ctx, bit_index)],
                    send_sem=grad_send_sem.at[bit_index],
                    recv_sem=grad_recv.at[bit_index],
                    device_id={"ctx": peer},
                    device_id_type=MESH,
                ).start()

    for bit_index in range(ctx_bits):

        @pl.when(own_bit(bit_index))
        def _():
            grad_parts[bit_index, grad_slot(my_ctx, bit_index)] = grad_send[
                bit_index, part_rows(my_ctx), :
            ]

    @pl.loop(0, n_local)
    def _(head):
        columns = head_columns(head)
        for row in range(tiles):
            rows = slice(row * TILE, (row + 1) * TILE)
            reach = (row + 1) * TILE
            query = rows_in[QUERY, rows, columns]
            cot = rows_in[COT, rows, columns]
            keys = rows_in[KEY, 0:reach, columns]
            values = rows_in[VALUE, 0:reach, columns]
            scores = dot_nt(query, keys)
            dots = dot_nt(cot, values)
            probs, score_grads = [], []
            for column in range(row + 1):
                if column == row:
                    weight = jnp.zeros((TILE, TILE), jnp.float32)
                    for level_index in range(8):
                        weight = jnp.where(
                            levels[...] == level_index,
                            code_column(head, level_index, rows),
                            weight,
                        )
                else:
                    weight = code_column(head, 7 + (row ^ column).bit_length(), rows)
                at = slice(column * TILE, (column + 1) * TILE)
                probs.append((weight * scores[:, at]).astype(jnp.bfloat16))
                score_grads.append((weight * dots[:, at]).astype(jnp.bfloat16))
            probs = jnp.concatenate(probs, axis=1)
            score_grads = jnp.concatenate(score_grads, axis=1)
            local[0, rows, columns] = dot_nn(probs, values)
            local[1, rows, columns] = dot_nn(score_grads, keys)
            key_grad = dot_tn(score_grads, query)
            value_grad = dot_tn(probs, cot)
            if row:
                local[2, 0 : row * TILE, columns] += key_grad[: row * TILE]
                local[3, 0 : row * TILE, columns] += value_grad[: row * TILE]
            local[2, rows, columns] = key_grad[row * TILE :]
            local[3, rows, columns] = value_grad[row * TILE :]

    def send_out(slot):
        for step in range(1, n_head):
            peer = lax.rem(my_head + step, n_head)
            pltpu.make_async_remote_copy(
                src_ref=rows_out.at[slot, share_rows(peer), :],
                dst_ref=outputs[slot].at[:, width_columns(my_head)],
                send_sem=out_send.at[slot],
                recv_sem=out_recv.at[slot],
                device_id={"head": peer},
                device_id_type=MESH,
            ).start()
        pltpu.make_async_copy(
            rows_out.at[slot, share_rows(my_head), :],
            outputs[slot].at[:, width_columns(my_head)],
            own_sem.at[4 + slot],
        ).start()

    for bit_index in range(ctx_bits):
        half = n_ctx // 2

        @pl.when(own_bit(bit_index))
        def _():
            others = grad_parts.at[bit_index, 0 : half - 1]
            pltpu.make_async_copy(others, others, grad_recv.at[bit_index]).wait()

        @pl.when(jnp.logical_not(own_bit(bit_index)))
        def _():
            others = grad_parts.at[bit_index]
            pltpu.make_async_copy(others, others, grad_recv.at[bit_index]).wait()

    upper = []
    for bit_index in range(ctx_bits):
        terms = grad_parts[bit_index].astype(jnp.float32)
        upper.append(
            jnp.sum(terms.reshape(n_ctx // 2 ** (bit_index + 1), 2**bit_index, part, TILE), axis=1)
        )
    for block in range(n_ctx):
        total = jnp.zeros((part, TILE), jnp.float32)
        for bit_index in range(ctx_bits):
            if not block >> bit_index & 1:
                total = total + upper[bit_index][block >> (bit_index + 1)]
        pulled_send[block] = total.astype(jnp.bfloat16)

    @pl.loop(1, n_ctx)
    def _(step):
        peer = ctx_peer(step)
        pltpu.make_async_remote_copy(
            src_ref=pulled_send.at[peer],
            dst_ref=pulled.at[part_rows(my_ctx), :],
            send_sem=pulled_sems.at[0],
            recv_sem=pulled_sems.at[1],
            device_id={"ctx": peer},
            device_id_type=MESH,
        ).start()

    pulled[part_rows(my_ctx), :] = pulled_send[my_ctx]

    for bit_index in range(ctx_bits):

        @pl.when(own_bit(bit_index))
        def _():
            others = bucket.at[bit_index, 0 : state_rows - part, :]
            pltpu.make_async_copy(others, others, bucket_recv.at[bit_index]).wait()

    @pl.loop(0, n_local)
    def _(head):
        columns = head_columns(head)
        for row in range(tiles):
            rows = slice(row * TILE, (row + 1) * TILE)
            query = rows_in[QUERY, rows, columns]
            cot = rows_in[COT, rows, columns]
            attended = local[0, rows, columns]
            grad_query = local[1, rows, columns]
            for bit_index in range(ctx_bits):
                row_scale = code_column(head, tok_bits + 1 + bit_index, rows)
                states = bucket[bit_index, columns, :]
                attended = attended + row_scale * dot_nn(query, states)
                grad_query = grad_query + row_scale * dot_nt(cot, states)
            rows_out[0, rows, columns] = attended.astype(jnp.bfloat16)
            rows_out[1, rows, columns] = grad_query.astype(jnp.bfloat16)

    send_out(0)
    send_out(1)

    pulled_others = pulled.at[0 : state_rows - part, :]
    pltpu.make_async_copy(pulled_others, pulled_others, pulled_sems.at[1]).wait()

    @pl.loop(0, n_local)
    def _(head):
        columns = head_columns(head)
        states = pulled[columns, :]
        grad_key = local[2, :, columns] + dot_nt(rows_in[VALUE, :, columns], states)
        rows_out[2, :, columns] = grad_key.astype(jnp.bfloat16)
        grad_value = local[3, :, columns] + dot_nn(rows_in[KEY, :, columns], states)
        rows_out[3, :, columns] = grad_value.astype(jnp.bfloat16)

    send_out(2)
    send_out(3)

    for slot in range(4):
        sent = rows_in.at[slot, 0 : length - share, :]
        pltpu.make_async_copy(sent, sent, in_send.at[slot]).wait()
    pltpu.make_async_copy(state_others, state_others, state_sems.at[0]).wait()
    pltpu.make_async_copy(pulled_others, pulled_others, pulled_sems.at[0]).wait()
    for bit_index in range(ctx_bits):
        half = n_ctx // 2
        rest = grad_parts.at[bit_index, 0 : half - 1]

        @pl.when(own_bit(bit_index))
        def _():
            pltpu.make_async_copy(rest, rest, bucket_send_sem.at[bit_index]).wait()
            sent = grad_send.at[bit_index, 0 : state_rows - part, :]
            pltpu.make_async_copy(sent, sent, grad_send_sem.at[bit_index]).wait()

        @pl.when(jnp.logical_not(own_bit(bit_index)))
        def _():
            sent = grad_parts.at[bit_index]
            pltpu.make_async_copy(sent, sent, bucket_send_sem.at[bit_index]).wait()

    for slot in range(4):
        sent = rows_out.at[slot, 0 : length - share, :]
        pltpu.make_async_copy(sent, sent, out_send.at[slot]).wait()
        pltpu.make_async_copy(sent, sent, out_recv.at[slot]).wait()
        pltpu.make_async_copy(
            rows_out.at[slot, share_rows(my_head), :],
            outputs[slot].at[:, width_columns(my_head)],
            own_sem.at[4 + slot],
        ).wait()


def on_device(n_ctx, n_head, query_input, key_input, value_input, cotangent, level_codes):
    share, features = query_input.shape
    n_local, n_levels, length = level_codes.shape
    width = features // n_head
    tok_bits = length.bit_length() - 1
    ctx_bits = n_levels - tok_bits - 1
    state_rows = n_local * TILE
    part = state_rows // n_ctx
    half = jnp.bfloat16
    result = jax.ShapeDtypeStruct((share, features), half)
    dma = pltpu.SemaphoreType.DMA
    return pl.pallas_call(
        functools.partial(kernel, n_ctx, n_head, ctx_bits, tok_bits),
        out_shape=(result,) * 4,
        in_specs=[pl.BlockSpec(memory_space=pl.ANY)] * 5,
        out_specs=(pl.BlockSpec(memory_space=pl.ANY),) * 4,
        scratch_shapes=[
            pltpu.VMEM((4, length, width), half),
            pltpu.VMEM(level_codes.shape, jnp.int32),
            pltpu.VMEM((TILE, length), jnp.float32),
            pltpu.VMEM((n_local, length, TILE), jnp.float32),
            pltpu.VMEM((TILE, TILE), jnp.int32),
            pltpu.VMEM((4, length, width), jnp.float32),
            pltpu.VMEM((4, length, width), half),
            pltpu.VMEM((state_rows, TILE), half),
            pltpu.VMEM((n_ctx, part, TILE), half),
            pltpu.VMEM((n_ctx, part, TILE), half),
            pltpu.VMEM((ctx_bits, state_rows, TILE), half),
            pltpu.VMEM((ctx_bits, state_rows, TILE), half),
            pltpu.VMEM((ctx_bits, n_ctx // 2, part, TILE), half),
            pltpu.VMEM((n_ctx, part, TILE), half),
            pltpu.VMEM((state_rows, TILE), half),
            dma((4,)),
            dma((4,)),
            dma((9,)),
            dma((2,)),
            dma((ctx_bits,)),
            dma((ctx_bits,)),
            dma((ctx_bits,)),
            dma((ctx_bits,)),
            dma((2,)),
            dma((4,)),
            dma((4,)),
        ],
        compiler_params=pltpu.CompilerParams(collective_id=0, has_side_effects=True),
        name="layer",
    )(query_input, key_input, value_input, cotangent, level_codes)


def solution(mesh):
    rows = P(("ctx", "head"), None)
    return jax.shard_map(
        functools.partial(on_device, mesh.shape["ctx"], mesh.shape["head"]),
        mesh=mesh,
        in_specs=(rows, rows, rows, rows, P("head", None, "ctx")),
        out_specs=(rows, rows, rows, rows),
        check_vma=False,
    )
```

time: 214 us -> 90.3 us (0.42)
  Pallas kernels: 0 us -> 81.5 us
  waiting for transfers between devices: 73.3 us -> 0 us
  starting transfers between devices: 63.8 us -> 0 us
  matrix products: 29.9 us -> 0 us
  local copies, waits for them, and re-layouts: 32.1 us -> 6.78 us
  other arithmetic: 12.1 us -> 0 us
    pallas_call x0 -> x1, Pallas kernels: none -> 81.5 us  [on_device(): pl.pallas_call(functools.partial(kernel, n_ctx, n_head, ctx_bits, tok_bit...]
    all_to_all x8 -> x0, starting transfers between devices: 44.2 us -> none  [the longest x1 9.64 us: on_device(): lax.all_to_all(attended, 'head', split_axis=0, concat_axis=1, tiled=True)]
    all_to_all x8 -> x0, waiting for transfers between devices: 37.6 us -> none  [the longest x1 8.33 us: on_device(): lax.all_to_all(value_input, 'head', split_axis=1, concat_axis=0, tiled=True)]
    ppermute x10 -> x0, waiting for transfers between devices: 35.7 us -> none  [swapped(): return lax.ppermute(block, axis, route)]
    dot_general x12 -> x0, matrix products: 29.9 us -> none  [the longest x1 7.41 us: row_step(): jnp.einsum('phe,she->hps', cot_heads, value_heads, preferred_element_type...]
    ppermute x10 -> x0, starting transfers between devices: 19.5 us -> none  [swapped(): return lax.ppermute(block, axis, route)]
    all_to_all x10 -> x0, local copies, waits for them, and re-layouts: 14 us -> none  [the longest x2 3.91 us: on_device(): lax.all_to_all(grad_key, 'head', split_axis=0, concat_axis=1, tiled=True)]
    convert_element_type x7 -> x0, local copies, waits for them, and re-layouts: 9.39 us -> none  [the longest x2 3.24 us: on_device(): (local_qgrad + cross_qgrad).astype(jnp.bfloat16).reshape(flat_shape)]
  transfers between devices with their start and end apart: 18 -> 0, of which waited for: 14 -> 0; matrix products, arithmetic and copies ran while one was open for 30% -> 0% of each run, Pallas kernels for 0% -> 0%
where the time goes in v1:
time: 90.3 us; the launch traced here: 89 us
  Pallas kernels  81.5 us (90%)
  local copies, waits for them, and re-layouts  6.78 us (8%)
    pallas_call x1, Pallas kernels, on_device(): pl.pallas_call(functools.partial(kernel, n_ctx, n_head, ctx_bits, tok_bit...  81.5 us
    unnamed x11, local copies, waits for them, and re-layouts  6.78 us

profile of v1, /device:TPU:1, one launch (start us, length us, event | category | flops | bytes accessed | tf_op | source)
XLA Modules:
  0.0 89.0 jit_solution(13331636677359317586)
XLA Ops:
  0.6 1.6 %copy.9.codes_ref = s32[4,15,512]{2,1,0:T(8,128)} copy(s32[4,15,512]{2,0,1:T(4,128)} %param.9) | data formatting | bytes 245760 | tf_op args[4]
  2.2 81.5 %layer.1 = (bf16[64,4096]{1,0:T(8,128)(2,1)}, bf16[64,4096]{1,0:T(8,128)(2,1)}, bf16[64,4096]{1,0:T(8,128)(2,1)}, bf16[64,4096]{1,0:T(8,128)(2,1)}) custom-call(bf16[64,4096]{1,0:T(8,128)(2,1)} %query_ref.1, bf16[64,4096]{1,0:T(8,128)(2,1)} %key_ref.1, bf16[64,4096]{1,0:T(8,128)(2,1)} %value_ref.1, bf16[64,4096]{1,0:T(8,128)(2,1)} %cot_ref.1, ...), custom_call_target="tpu_custom_call" | custom-call | tf_op jit(solution)/shard_map/layer/pallas_call | solution.py:451
  83.8 0.0 copy-start.2
  83.8 1.9 %copy.14 = bf16[64,4096]{1,0:T(8,128)(2,1)} copy(bf16[64,4096]{1,0:T(8,128)(2,1)} %get-tuple-element.8) | data formatting | bytes 1048576
  85.7 0.0 copy-done.2
  85.7 0.0 copy-start.1
  85.7 0.8 copy.15
  86.5 0.4 copy-done.1
  86.9 0.0 copy-start
  86.9 0.8 copy.16
  87.7 0.4 copy-done
  88.2 0.8 copy.17
Async XLA Ops:
  83.8 1.9 %copy-start.2 = (bf16[64,4096]{1,0:T(8,128)(2,1)S(1)}, bf16[64,4096]{1,0:T(8,128)(2,1)}, u32[]{:S(2)}) copy-start(bf16[64,4096]{1,0:T(8,128)(2,1)} %get-tuple-element.9) | copy-start | bytes 1572868
  85.7 1.2 %copy-start.1 = (bf16[64,4096]{1,0:T(8,128)(2,1)S(1)}, bf16[64,4096]{1,0:T(8,128)(2,1)}, u32[]{:S(2)}) copy-start(bf16[64,4096]{1,0:T(8,128)(2,1)} %get-tuple-element.10) | copy-start | bytes 1572868
  86.9 1.2 %copy-start = (bf16[64,4096]{1,0:T(8,128)(2,1)S(1)}, bf16[64,4096]{1,0:T(8,128)(2,1)}, u32[]{:S(2)}) copy-start(bf16[64,4096]{1,0:T(8,128)(2,1)} %get-tuple-element.11) | copy-start | bytes 1572868

commit v2 on v1

--- a/solution.py
+++ b/solution.py
@@ -44,11 +44,14 @@
     gq_ref,
     gk_ref,
     gv_ref,
+    staged,
     rows_in,
     codes,
     code_rows,
     code_cols,
     levels,
+    probs,
+    score_grads,
     local,
     rows_out,
     state_send,
@@ -59,6 +62,7 @@
     grad_parts,
     pulled_send,
     pulled,
+    stage_sem,
     in_send,
     in_recv,
     own_sem,
@@ -115,7 +119,7 @@
     def _(step):
         pl.semaphore_signal(barrier, inc=1, device_id={"ctx": ctx_peer(step)}, device_id_type=MESH)
 
-    codes_copy = pltpu.make_async_copy(codes_ref, codes, own_sem.at[8])
+    codes_copy = pltpu.make_async_copy(codes_ref, codes, own_sem.at[4])
     codes_copy.start()
     for slot, array in enumerate(inputs):
         pltpu.make_async_copy(
@@ -123,13 +127,15 @@
             rows_in.at[slot, share_rows(my_head), :],
             own_sem.at[slot],
         ).start()
+        pltpu.make_async_copy(array, staged.at[slot], stage_sem.at[slot]).start()
     pl.semaphore_wait(barrier, n_head - 1 + n_ctx - 1)
 
     for slot, array in enumerate(inputs):
+        pltpu.make_async_copy(array, staged.at[slot], stage_sem.at[slot]).wait()
         for step in range(1, n_head):
             peer = lax.rem(my_head + step, n_head)
             pltpu.make_async_remote_copy(
-                src_ref=array.at[:, width_columns(peer)],
+                src_ref=staged.at[slot, :, width_columns(peer)],
                 dst_ref=rows_in.at[slot, share_rows(my_head), :],
                 send_sem=in_send.at[slot],
                 recv_sem=in_recv.at[slot],
@@ -140,7 +146,7 @@
     codes_copy.wait()
     for head in range(n_local):
         code_rows[...] = jnp.zeros_like(code_rows)
-        code_rows[0 : codes.shape[1], :] = codes[head].astype(jnp.float32)
+        code_rows[0 : codes.shape[0], :] = codes[:, head, :].astype(jnp.float32)
         code_cols[head] = code_rows[...].T
     place = lax.broadcasted_iota(jnp.int32, (TILE, TILE), 0)
     other = lax.broadcasted_iota(jnp.int32, (TILE, TILE), 1)
@@ -168,6 +174,49 @@
         return code_cols[head, rows, level_index : level_index + 1] * (
             level_gain(level_index) * scale / 8.0
         )
+
+    def weighted(head, row, products):
+        rows = slice(row * TILE, (row + 1) * TILE)
+        pieces = []
+        for column in range(row + 1):
+            if column == row:
+                weight = jnp.zeros((TILE, TILE), jnp.float32)
+                for level_index in range(8):
+                    weight = jnp.where(
+                        levels[...] == level_index, code_column(head, level_index, rows), weight
+                    )
+            else:
+                weight = code_column(head, 7 + (row ^ column).bit_length(), rows)
+            at = slice(column * TILE, (column + 1) * TILE)
+            pieces.append((weight * products[:, at]).astype(jnp.bfloat16))
+        return jnp.concatenate(pieces, axis=1)
+
+    def attend(head):
+        columns = head_columns(head)
+        for row in range(tiles):
+            rows, reach = slice(row * TILE, (row + 1) * TILE), (row + 1) * TILE
+            scores = dot_nt(rows_in[QUERY, rows, columns], rows_in[KEY, 0:reach, columns])
+            pairs = weighted(head, row, scores)
+            probs[head, rows, 0:reach] = pairs
+            local[0, rows, columns] = dot_nn(pairs, rows_in[VALUE, 0:reach, columns])
+
+    def attend_back(head):
+        columns = head_columns(head)
+        for row in range(tiles):
+            rows, reach = slice(row * TILE, (row + 1) * TILE), (row + 1) * TILE
+            dots = dot_nt(rows_in[COT, rows, columns], rows_in[VALUE, 0:reach, columns])
+            pairs = weighted(head, row, dots)
+            score_grads[head, rows, 0:reach] = pairs
+            local[1, rows, columns] = dot_nn(pairs, rows_in[KEY, 0:reach, columns])
+
+    def sum_back(head):
+        columns = head_columns(head)
+        for column in range(tiles):
+            at, below = slice(column * TILE, (column + 1) * TILE), slice(column * TILE, length)
+            local[2, at, columns] = dot_tn(
+                score_grads[head, below, at], rows_in[QUERY, below, columns]
+            )
+            local[3, at, columns] = dot_tn(probs[head, below, at], rows_in[COT, below, columns])
 
     arrived(KEY)
     arrived(VALUE)
@@ -191,6 +240,8 @@
         ).start()
 
     state_parts[my_ctx] = state_send[part_rows(my_ctx), :]
+    arrived(QUERY)
+    pl.loop(0, n_local // 2)(attend)
     state_others = state_parts.at[0 : n_ctx - 1]
     pltpu.make_async_copy(state_others, state_others, state_sems.at[1]).wait()
 
@@ -228,18 +279,22 @@
                 first_node[bit_index] + my_ctx // 2 ** (bit_index + 1)
             ]
 
-    arrived(QUERY)
+    pl.loop(n_local // 2, n_local)(attend)
     arrived(COT)
 
     @pl.loop(0, n_local)
     def _(head):
         columns = head_columns(head)
-        query = rows_in[QUERY, :, columns]
         cot = rows_in[COT, :, columns].astype(jnp.float32)
+        scaled = [
+            (code_column(head, tok_bits + 1 + bit_index, slice(None)) * cot).astype(jnp.bfloat16)
+            for bit_index in range(ctx_bits)
+        ]
+        grads = dot_tn(rows_in[QUERY, :, columns], jnp.concatenate(scaled, axis=1))
         for bit_index in range(ctx_bits):
-            row_scale = code_column(head, tok_bits + 1 + bit_index, slice(None))
-            scaled = (row_scale * cot).astype(jnp.bfloat16)
-            grad_send[bit_index, columns, :] = dot_tn(query, scaled).astype(jnp.bfloat16)
+            grad_send[bit_index, columns, :] = grads[
+                :, bit_index * TILE : (bit_index + 1) * TILE
+            ].astype(jnp.bfloat16)
 
     def grad_slot(block, bit_index):
         return block // 2 ** (bit_index + 1) * 2**bit_index + block % 2**bit_index
@@ -268,61 +323,51 @@
                 bit_index, part_rows(my_ctx), :
             ]
 
-    @pl.loop(0, n_local)
-    def _(head):
-        columns = head_columns(head)
-        for row in range(tiles):
-            rows = slice(row * TILE, (row + 1) * TILE)
-            reach = (row + 1) * TILE
-            query = rows_in[QUERY, rows, columns]
-            cot = rows_in[COT, rows, columns]
-            keys = rows_in[KEY, 0:reach, columns]
-            values = rows_in[VALUE, 0:reach, columns]
-            scores = dot_nt(query, keys)
-            dots = dot_nt(cot, values)
-            probs, score_grads = [], []
-            for column in range(row + 1):
-                if column == row:
-                    weight = jnp.zeros((TILE, TILE), jnp.float32)
-                    for level_index in range(8):
-                        weight = jnp.where(
-                            levels[...] == level_index,
-                            code_column(head, level_index, rows),
-                            weight,
-                        )
-                else:
-                    weight = code_column(head, 7 + (row ^ column).bit_length(), rows)
-                at = slice(column * TILE, (column + 1) * TILE)
-                probs.append((weight * scores[:, at]).astype(jnp.bfloat16))
-                score_grads.append((weight * dots[:, at]).astype(jnp.bfloat16))
-            probs = jnp.concatenate(probs, axis=1)
-            score_grads = jnp.concatenate(score_grads, axis=1)
-            local[0, rows, columns] = dot_nn(probs, values)
-            local[1, rows, columns] = dot_nn(score_grads, keys)
-            key_grad = dot_tn(score_grads, query)
-            value_grad = dot_tn(probs, cot)
-            if row:
-                local[2, 0 : row * TILE, columns] += key_grad[: row * TILE]
-                local[3, 0 : row * TILE, columns] += value_grad[: row * TILE]
-            local[2, rows, columns] = key_grad[row * TILE :]
-            local[3, rows, columns] = value_grad[row * TILE :]
-
-    def send_out(slot):
+    pl.loop(0, n_local)(attend_back)
+    pl.loop(0, n_local)(sum_back)
+
+    def send_out(slot, columns_of, columns):
         for step in range(1, n_head):
             peer = lax.rem(my_head + step, n_head)
             pltpu.make_async_remote_copy(
-                src_ref=rows_out.at[slot, share_rows(peer), :],
-                dst_ref=outputs[slot].at[:, width_columns(my_head)],
+                src_ref=rows_out.at[slot, share_rows(peer), columns],
+                dst_ref=outputs[slot].at[:, columns_of],
                 send_sem=out_send.at[slot],
                 recv_sem=out_recv.at[slot],
                 device_id={"head": peer},
                 device_id_type=MESH,
             ).start()
-        pltpu.make_async_copy(
-            rows_out.at[slot, share_rows(my_head), :],
-            outputs[slot].at[:, width_columns(my_head)],
-            own_sem.at[4 + slot],
-        ).start()
+        outputs[slot][:, columns_of] = rows_out[slot, share_rows(my_head), columns]
+
+    def out_columns(head):
+        return pl.ds(pl.multiple_of(my_head * width + head * TILE, TILE), TILE)
+
+    for bit_index in range(ctx_bits):
+
+        @pl.when(own_bit(bit_index))
+        def _():
+            others = bucket.at[bit_index, 0 : state_rows - part, :]
+            pltpu.make_async_copy(others, others, bucket_recv.at[bit_index]).wait()
+
+    @pl.loop(0, n_local)
+    def _(head):
+        columns = head_columns(head)
+        states = [bucket[bit_index, columns, :] for bit_index in range(ctx_bits)]
+        wide, tall = jnp.concatenate(states, axis=1), jnp.concatenate(states, axis=0)
+        for row in range(tiles):
+            rows = slice(row * TILE, (row + 1) * TILE)
+            attended, grad_query = local[0, rows, columns], local[1, rows, columns]
+            reads = dot_nn(rows_in[QUERY, rows, columns], wide)
+            cot_reads = dot_nt(rows_in[COT, rows, columns], tall)
+            for bit_index in range(ctx_bits):
+                row_scale = code_column(head, tok_bits + 1 + bit_index, rows)
+                at = slice(bit_index * TILE, (bit_index + 1) * TILE)
+                attended = attended + row_scale * reads[:, at]
+                grad_query = grad_query + row_scale * cot_reads[:, at]
+            rows_out[0, rows, columns] = attended.astype(jnp.bfloat16)
+            rows_out[1, rows, columns] = grad_query.astype(jnp.bfloat16)
+        send_out(0, out_columns(head), columns)
+        send_out(1, out_columns(head), columns)
 
     for bit_index in range(ctx_bits):
         half = n_ctx // 2
@@ -364,33 +409,6 @@
 
     pulled[part_rows(my_ctx), :] = pulled_send[my_ctx]
 
-    for bit_index in range(ctx_bits):
-
-        @pl.when(own_bit(bit_index))
-        def _():
-            others = bucket.at[bit_index, 0 : state_rows - part, :]
-            pltpu.make_async_copy(others, others, bucket_recv.at[bit_index]).wait()
-
-    @pl.loop(0, n_local)
-    def _(head):
-        columns = head_columns(head)
-        for row in range(tiles):
-            rows = slice(row * TILE, (row + 1) * TILE)
-            query = rows_in[QUERY, rows, columns]
-            cot = rows_in[COT, rows, columns]
-            attended = local[0, rows, columns]
-            grad_query = local[1, rows, columns]
-            for bit_index in range(ctx_bits):
-                row_scale = code_column(head, tok_bits + 1 + bit_index, rows)
-                states = bucket[bit_index, columns, :]
-                attended = attended + row_scale * dot_nn(query, states)
-                grad_query = grad_query + row_scale * dot_nt(cot, states)
-            rows_out[0, rows, columns] = attended.astype(jnp.bfloat16)
-            rows_out[1, rows, columns] = grad_query.astype(jnp.bfloat16)
-
-    send_out(0)
-    send_out(1)
-
     pulled_others = pulled.at[0 : state_rows - part, :]
     pltpu.make_async_copy(pulled_others, pulled_others, pulled_sems.at[1]).wait()
 
@@ -402,9 +420,8 @@
         rows_out[2, :, columns] = grad_key.astype(jnp.bfloat16)
         grad_value = local[3, :, columns] + dot_nn(rows_in[KEY, :, columns], states)
         rows_out[3, :, columns] = grad_value.astype(jnp.bfloat16)
-
-    send_out(2)
-    send_out(3)
+        send_out(2, out_columns(head), columns)
+        send_out(3, out_columns(head), columns)
 
     for slot in range(4):
         sent = rows_in.at[slot, 0 : length - share, :]
@@ -430,11 +447,26 @@
         sent = rows_out.at[slot, 0 : length - share, :]
         pltpu.make_async_copy(sent, sent, out_send.at[slot]).wait()
         pltpu.make_async_copy(sent, sent, out_recv.at[slot]).wait()
-        pltpu.make_async_copy(
-            rows_out.at[slot, share_rows(my_head), :],
-            outputs[slot].at[:, width_columns(my_head)],
-            own_sem.at[4 + slot],
-        ).wait()
+
+
+def put_out_kernel(*refs):
+    held, results, sems = refs[:4], refs[4:8], refs[8]
+    copies = [pltpu.make_async_copy(held[i], results[i], sems.at[i]) for i in range(4)]
+    for copy in copies:
+        copy.start()
+    for copy in copies:
+        copy.wait()
+
+
+def put_out(held):
+    return pl.pallas_call(
+        put_out_kernel,
+        out_shape=tuple(jax.ShapeDtypeStruct(array.shape, array.dtype) for array in held),
+        in_specs=[pl.BlockSpec(memory_space=pltpu.VMEM)] * 4,
+        out_specs=(pl.BlockSpec(memory_space=pl.ANY),) * 4,
+        scratch_shapes=[pltpu.SemaphoreType.DMA((4,))],
+        name="put_out",
+    )(*held)
 
 
 def on_device(n_ctx, n_head, query_input, key_input, value_input, cotangent, level_codes):
@@ -446,19 +478,21 @@
     state_rows = n_local * TILE
     part = state_rows // n_ctx
     half = jnp.bfloat16
-    result = jax.ShapeDtypeStruct((share, features), half)
     dma = pltpu.SemaphoreType.DMA
-    return pl.pallas_call(
+    held = pl.pallas_call(
         functools.partial(kernel, n_ctx, n_head, ctx_bits, tok_bits),
-        out_shape=(result,) * 4,
+        out_shape=(pltpu.VMEM(query_input.shape, half),) * 4,
         in_specs=[pl.BlockSpec(memory_space=pl.ANY)] * 5,
-        out_specs=(pl.BlockSpec(memory_space=pl.ANY),) * 4,
+        out_specs=(pl.BlockSpec(memory_space=pltpu.VMEM),) * 4,
         scratch_shapes=[
+            pltpu.VMEM((4, share, features), half),
             pltpu.VMEM((4, length, width), half),
-            pltpu.VMEM(level_codes.shape, jnp.int32),
+            pltpu.VMEM((n_levels, n_local, length), jnp.int32),
             pltpu.VMEM((TILE, length), jnp.float32),
             pltpu.VMEM((n_local, length, TILE), jnp.float32),
             pltpu.VMEM((TILE, TILE), jnp.int32),
+            pltpu.VMEM((n_local, length, length), half),
+            pltpu.VMEM((n_local, length, length), half),
             pltpu.VMEM((4, length, width), jnp.float32),
             pltpu.VMEM((4, length, width), half),
             pltpu.VMEM((state_rows, TILE), half),
@@ -471,7 +505,8 @@
             pltpu.VMEM((state_rows, TILE), half),
             dma((4,)),
             dma((4,)),
-            dma((9,)),
+            dma((4,)),
+            dma((5,)),
             dma((2,)),
             dma((ctx_bits,)),
             dma((ctx_bits,)),
@@ -483,7 +518,8 @@
         ],
         compiler_params=pltpu.CompilerParams(collective_id=0, has_side_effects=True),
         name="layer",
-    )(query_input, key_input, value_input, cotangent, level_codes)
+    )(query_input, key_input, value_input, cotangent, jnp.transpose(level_codes, (1, 0, 2)))
+    return put_out([pltpu.with_memory_space_constraint(array, pltpu.VMEM) for array in held])
 
 
 def solution(mesh):

time: 90.3 us -> 77.8 us (0.86); the launches traced: 89 us -> 77.7 us
  local copies, waits for them, and re-layouts: 6.78 us -> 0 us
  Pallas kernels: 81.5 us -> 77 us
    unnamed x11 -> x0, local copies, waits for them, and re-layouts: 6.78 us -> none
    pallas_call x1, Pallas kernels: 81.5 us -> 75.7 us  [on_device(): pl.pallas_call(functools.partial(kernel, n_ctx, n_head, ctx_bits, tok_bit...]
    pallas_call x0 -> x1, Pallas kernels: none -> 1.35 us  [put_out(): pl.pallas_call(put_out_kernel, out_shape=tuple((jax.ShapeDtypeStruct(arra...]
where the time goes in v2:
time: 77.8 us; the launch traced here: 77.7 us
  Pallas kernels  77 us (99%)
    pallas_call x1, Pallas kernels, on_device(): pl.pallas_call(functools.partial(kernel, n_ctx, n_head, ctx_bits, tok_bit...  75.7 us

profile of v2, /device:TPU:1, one launch (start us, length us, event | category | flops | bytes accessed | tf_op | source)
XLA Modules:
  0.0 77.7 jit_solution(14918261128014386004)
XLA Ops:
  0.6 75.7 %layer.1 = (bf16[64,4096]{1,0:T(8,128)(2,1)S(1)}, bf16[64,4096]{1,0:T(8,128)(2,1)S(1)}, bf16[64,4096]{1,0:T(8,128)(2,1)S(1)}, bf16[64,4096]{1,0:T(8,128)(2,1)S(1)}) custom-call(bf16[64,4096]{1,0:T(8,128)(2,1)} %query_ref.1, bf16[64,4096]{1,0:T(8,128)(2,1)} %key_ref.1, bf16[64,4096]{1,0:T(8,128)(2,1)} %value_ref.1, bf16[64,4096]{1,0:T(8,128)(2,1)} %cot_ref.1, ...), custom_call_target="tpu_custom_call" | custom-call | tf_op jit(solution)/shard_map/layer/pallas_call | solution.py:482
  76.3 1.3 %put_out.1 = (bf16[64,4096]{1,0:T(8,128)(2,1)}, bf16[64,4096]{1,0:T(8,128)(2,1)}, bf16[64,4096]{1,0:T(8,128)(2,1)}, bf16[64,4096]{1,0:T(8,128)(2,1)}) custom-call(bf16[64,4096]{1,0:T(8,128)(2,1)S(1)} %get-tuple-element.8.refs_0_, bf16[64,4096]{1,0:T(8,128)(2,1)S(1)} %get-tuple-element.9.refs_1_, bf16[64,4096]{1,0:T(8,128)(2,1)S(1)} %get-tuple-element.10.refs_2_, ...), custom_call_target="tpu_custom_call" | custom-call | tf_op jit(solution)/shard_map/put_out/pallas_call | solution.py:462

commit v3 on v2

v3 whole, which is shorter than its diff:
```python
import functools

import jax
import jax.numpy as jnp
from jax import lax
from jax.experimental import pallas as pl
from jax.experimental.pallas import tpu as pltpu
from jax.sharding import PartitionSpec as P

MESH = pl.DeviceIdType.MESH
KEY, VALUE, QUERY, COT = range(4)
TILE = 128
UNITS = 2
Y_SIZE, Y_BITS = 4, 2


def level_gain(level):
    if level == 0:
        return 1.0
    return 2.0 ** (-(level - 1) / 2.0)


def dot_nn(a, b):
    return lax.dot_general(a, b, (((1,), (0,)), ((), ())), preferred_element_type=jnp.float32)


def dot_nt(a, b):
    return lax.dot_general(a, b, (((1,), (1,)), ((), ())), preferred_element_type=jnp.float32)


def dot_tn(a, b):
    return lax.dot_general(a, b, (((0,), (0,)), ((), ())), preferred_element_type=jnp.float32)


def kernel(
    n_ctx,
    n_head,
    ctx_bits,
    tok_bits,
    query_ref,
    key_ref,
    value_ref,
    cot_ref,
    codes_ref,
    out_ref,
    gq_ref,
    gk_ref,
    gv_ref,
    staged,
    rows_in,
    codes,
    code_rows,
    code_cols,
    levels,
    probs,
    score_grads,
    local,
    rows_out,
    state_send,
    state_parts,
    pair_send,
    plane_parts,
    above_send,
    bucket,
    grad_send,
    grad_parts,
    plane_grad_send,
    plane_grad_parts,
    pulled_send,
    pulled_half,
    pulled,
    next_grad,
    stage_sem,
    own_sem,
    in_send,
    in_recv,
    state_send_sem,
    state_recv,
    plane_send_sem,
    plane_recv,
    bucket_send_sem,
    bucket_recv,
    grad_send_sem,
    grad_recv,
    plane_grad_send_sem,
    plane_grad_recv,
    pulled_send_sem,
    pulled_recv,
    next_send_sem,
    next_recv,
    out_send,
    out_recv,
):
    my_ctx = lax.axis_index("ctx")
    my_head = lax.axis_index("head")
    my_y = lax.rem(my_ctx, Y_SIZE)
    my_z = my_ctx // Y_SIZE
    n_z = n_ctx // Y_SIZE
    z_bits = ctx_bits - Y_BITS
    inputs = (key_ref, value_ref, query_ref, cot_ref)
    outputs = (out_ref, gq_ref, gk_ref, gv_ref)
    share = query_ref.shape[0]
    length = share * n_head
    width = query_ref.shape[1] // n_head
    n_local = width // TILE
    unit_heads = n_local // UNITS
    unit_width = width // UNITS
    unit_rows = unit_heads * TILE
    part = unit_rows // Y_SIZE
    tiles = length // TILE
    scale = TILE ** (-0.5)
    f32, half = jnp.float32, jnp.bfloat16

    def z_bit(bit_index):
        return my_z // 2**bit_index % 2 == 1

    def group_start(bit_index):
        return my_z // 2 ** (bit_index + 1) * 2 ** (bit_index + 1)

    def y_peer(step):
        return lax.rem(my_y + step, Y_SIZE)

    def at_y(y):
        return {"ctx": my_z * Y_SIZE + y}

    def at_z(z):
        return {"ctx": z * Y_SIZE + my_y}

    def head_columns(head):
        return pl.ds(pl.multiple_of(head * TILE, TILE), TILE)

    def unit_range(unit):
        return slice(unit * unit_rows, (unit + 1) * unit_rows)

    def part_rows(unit, owner):
        return pl.ds(pl.multiple_of(unit * unit_rows + owner * part, part), part)

    def share_rows(owner):
        return pl.ds(pl.multiple_of(owner * share, share), share)

    def unit_columns(owner, unit):
        return pl.ds(pl.multiple_of(owner * width + unit * unit_width, unit_width), unit_width)

    def send(src, dst, send_sem, recv_sem, device):
        pltpu.make_async_remote_copy(
            src_ref=src,
            dst_ref=dst,
            send_sem=send_sem,
            recv_sem=recv_sem,
            device_id=device,
            device_id_type=MESH,
        ).start()

    def wait(bytes_of, sem):
        pltpu.make_async_copy(bytes_of, bytes_of, sem).wait()

    barrier = pltpu.get_barrier_semaphore()

    def greet(device):
        pl.semaphore_signal(barrier, inc=1, device_id=device, device_id_type=MESH)

    for step in range(1, n_z):
        greet(at_z(lax.rem(my_z + step, n_z)))
    for step in range(1, Y_SIZE):
        greet(at_y(y_peer(step)))
    for step in range(1, n_head):
        greet({"head": lax.rem(my_head + step, n_head)})
    for slot, array in enumerate(inputs):
        pltpu.make_async_copy(array, staged.at[slot], stage_sem.at[slot]).start()
    codes_copy = pltpu.make_async_copy(codes_ref, codes, own_sem.at[0])
    codes_copy.start()
    with jax.named_scope("s_barrier"):
        pl.semaphore_wait(barrier, n_head - 1 + n_z - 1 + Y_SIZE - 1)

    for slot, array in enumerate(inputs):
        pltpu.make_async_copy(array, staged.at[slot], stage_sem.at[slot]).wait()
    for unit in range(UNITS):
        for slot in range(4):
            for step in range(1, n_head):
                peer = lax.rem(my_head + step, n_head)
                send(
                    staged.at[slot, :, unit_columns(peer, unit)],
                    rows_in.at[slot, share_rows(my_head), unit_columns(0, unit)],
                    in_send.at[slot, unit],
                    in_recv.at[slot, unit],
                    {"head": peer},
                )

    for slot in range(4):
        rows_in[slot, share_rows(my_head), :] = staged[
            slot, :, pl.ds(pl.multiple_of(my_head * width, width), width)
        ]
    codes_copy.wait()
    for head in range(n_local):
        code_rows[...] = jnp.zeros_like(code_rows)
        code_rows[0 : codes.shape[0], :] = codes[:, head, :].astype(f32)
        code_cols[head] = code_rows[...].T
    place = lax.broadcasted_iota(jnp.int32, (TILE, TILE), 0)
    other = lax.broadcasted_iota(jnp.int32, (TILE, TILE), 1)
    differ = place ^ other
    level = jnp.zeros((TILE, TILE), jnp.int32)
    for bit_index in range(7):
        level = level + (differ >= 2**bit_index).astype(jnp.int32)
    levels[...] = jnp.where(other <= place, level, -1)

    def is_clear(bit_index):
        return my_ctx // 2**bit_index % 2 == 0

    for bit_index in range(ctx_bits):

        @pl.when(is_clear(bit_index))
        def _():
            bucket[bit_index] = jnp.zeros((n_local * TILE, TILE), half)

    @pl.when(my_y % 2 == 1)
    def _():
        next_grad[...] = jnp.zeros_like(next_grad)

    def arrived(slot, unit):
        others = rows_in.at[slot, 0 : length - share, unit_columns(0, unit)]
        with jax.named_scope("s_in"):
            wait(others, in_recv.at[slot, unit])

    def code_column(head, level_index, rows):
        return code_cols[head, rows, level_index : level_index + 1] * (
            level_gain(level_index) * scale / 8.0
        )

    def weighted(head, row, products):
        rows = slice(row * TILE, (row + 1) * TILE)
        pieces = []
        for column in range(row + 1):
            if column == row:
                weight = jnp.zeros((TILE, TILE), f32)
                for level_index in range(8):
                    weight = jnp.where(
                        levels[...] == level_index, code_column(head, level_index, rows), weight
                    )
            else:
                weight = code_column(head, 7 + (row ^ column).bit_length(), rows)
            at = slice(column * TILE, (column + 1) * TILE)
            pieces.append((weight * products[:, at]).astype(half))
        return jnp.concatenate(pieces, axis=1)

    def each_head(unit, body):
        with jax.named_scope("c_" + body.__name__):
            pl.loop(unit * unit_heads, (unit + 1) * unit_heads)(body)

    def attend(head):
        columns = head_columns(head)
        for row in range(tiles):
            rows, reach = slice(row * TILE, (row + 1) * TILE), (row + 1) * TILE
            scores = dot_nt(rows_in[QUERY, rows, columns], rows_in[KEY, 0:reach, columns])
            pairs = weighted(head, row, scores)
            probs[head, rows, 0:reach] = pairs
            local[0, rows, columns] = dot_nn(pairs, rows_in[VALUE, 0:reach, columns])

    def attend_back(head):
        columns = head_columns(head)
        for row in range(tiles):
            rows, reach = slice(row * TILE, (row + 1) * TILE), (row + 1) * TILE
            dots = dot_nt(rows_in[COT, rows, columns], rows_in[VALUE, 0:reach, columns])
            pairs = weighted(head, row, dots)
            score_grads[head, rows, 0:reach] = pairs
            local[1, rows, columns] = dot_nn(pairs, rows_in[KEY, 0:reach, columns])

    def sum_back(head):
        columns = head_columns(head)
        for column in range(tiles):
            at, below = slice(column * TILE, (column + 1) * TILE), slice(column * TILE, length)
            local[2, at, columns] = dot_tn(
                score_grads[head, below, at], rows_in[QUERY, below, columns]
            )
            local[3, at, columns] = dot_tn(probs[head, below, at], rows_in[COT, below, columns])

    def state_of(head):
        columns = head_columns(head)
        state = dot_tn(rows_in[KEY, :, columns], rows_in[VALUE, :, columns])
        state_send[columns, :] = state.astype(half)

    def send_state(unit):
        each_head(unit, state_of)
        for step in range(1, Y_SIZE):
            peer = y_peer(step)
            send(
                state_send.at[part_rows(unit, peer), :],
                state_parts.at[unit, my_y],
                state_send_sem.at[unit],
                state_recv.at[unit],
                at_y(peer),
            )

        @pl.when(my_y % 2 == 0)
        def _():
            send(
                state_send.at[unit_range(unit), :],
                bucket.at[0, unit_range(unit), :],
                bucket_send_sem.at[unit, 0],
                bucket_recv.at[unit, 0],
                at_y(my_y + 1),
            )

        state_parts[unit, my_y] = state_send[part_rows(unit, my_y), :]

    def send_plane(unit):
        with jax.named_scope("s_state"):
            wait(state_parts.at[unit, 0 : Y_SIZE - 1], state_recv.at[unit])
        lower = state_parts[unit, 0].astype(f32) + state_parts[unit, 1].astype(f32)
        upper = state_parts[unit, 2].astype(f32) + state_parts[unit, 3].astype(f32)
        pair_send[unit, 0] = (lower + upper).astype(half)
        pair_send[unit, 1] = lower.astype(half)
        for step in range(1, n_z):

            @pl.when(my_z + step < n_z)
            def _():
                send(
                    pair_send.at[unit, 0],
                    plane_parts.at[unit, my_z],
                    plane_send_sem.at[unit, step],
                    plane_recv.at[unit, my_z],
                    at_z(my_z + step),
                )

        for y in (2, 3):

            @pl.when(my_y != y)
            def _():
                send(
                    pair_send.at[unit, 1],
                    bucket.at[1, part_rows(unit, my_y), :],
                    bucket_send_sem.at[unit, 1],
                    bucket_recv.at[unit, 1],
                    at_y(y),
                )

            @pl.when(my_y == y)
            def _():
                bucket[1, part_rows(unit, my_y), :] = pair_send[unit, 1]

    def send_above(unit):
        for z in range(n_z - 1):

            @pl.when(z < my_z)
            def _():
                with jax.named_scope("s_plane"):
                    wait(plane_parts.at[unit, z], plane_recv.at[unit, z])

        for bit_index in range(z_bits):

            @pl.when(z_bit(bit_index))
            def _():
                total = jnp.zeros((part, TILE), f32)
                for block in range(2**bit_index):
                    total = total + plane_parts[unit, group_start(bit_index) + block].astype(f32)
                above_send[unit, bit_index] = total.astype(half)
                for step in range(1, Y_SIZE):
                    send(
                        above_send.at[unit, bit_index],
                        bucket.at[Y_BITS + bit_index, part_rows(unit, my_y), :],
                        bucket_send_sem.at[unit, Y_BITS + bit_index],
                        bucket_recv.at[unit, Y_BITS + bit_index],
                        at_y(y_peer(step)),
                    )
                bucket[Y_BITS + bit_index, part_rows(unit, my_y), :] = above_send[unit, bit_index]

    def grad_of(head):
        columns = head_columns(head)
        cot = rows_in[COT, :, columns].astype(f32)
        scaled = [
            (code_column(head, tok_bits + 1 + bit_index, slice(None)) * cot).astype(half)
            for bit_index in range(ctx_bits)
        ]
        grads = dot_tn(rows_in[QUERY, :, columns], jnp.concatenate(scaled, axis=1))
        for bit_index in range(ctx_bits):
            grad_send[bit_index, columns, :] = grads[
                :, bit_index * TILE : (bit_index + 1) * TILE
            ].astype(half)

    def send_grad(unit):
        each_head(unit, grad_of)

        def parts(bit_index):
            for step in range(1, Y_SIZE):
                peer = y_peer(step)
                send(
                    grad_send.at[bit_index, part_rows(unit, peer), :],
                    grad_parts.at[unit, bit_index - 1, my_y],
                    grad_send_sem.at[unit, bit_index - 1],
                    grad_recv.at[unit, bit_index - 1],
                    at_y(peer),
                )
            grad_parts[unit, bit_index - 1, my_y] = grad_send[bit_index, part_rows(unit, my_y), :]

        for bit_index in range(z_bits):

            @pl.when(z_bit(bit_index))
            def _():
                parts(Y_BITS + bit_index)

        @pl.when(my_y >= 2)
        def _():
            parts(1)

        @pl.when(my_y % 2 == 1)
        def _():
            send(
                grad_send.at[0, unit_range(unit), :],
                next_grad.at[unit_range(unit), :],
                next_send_sem.at[unit],
                next_recv.at[unit],
                at_y(my_y - 1),
            )

    def send_plane_grad(unit):
        for bit_index in range(z_bits):

            @pl.when(z_bit(bit_index))
            def _():
                with jax.named_scope("s_grad"):
                    wait(
                        grad_parts.at[unit, 1 + bit_index, 0 : Y_SIZE - 1],
                        grad_recv.at[unit, 1 + bit_index],
                    )
                total = jnp.zeros((part, TILE), f32)
                for y in range(Y_SIZE):
                    total = total + grad_parts[unit, 1 + bit_index, y].astype(f32)
                plane_grad_send[unit, bit_index] = total.astype(half)
                for block in range(2**bit_index):
                    send(
                        plane_grad_send.at[unit, bit_index],
                        plane_grad_parts.at[unit, my_z],
                        plane_grad_send_sem.at[unit, 2**bit_index - 1 + block],
                        plane_grad_recv.at[unit, my_z],
                        at_z(group_start(bit_index) + block),
                    )

    def send_pulled(unit):
        @pl.when(my_y >= 2)
        def _():
            wait(grad_parts.at[unit, 0, 0:1], grad_recv.at[unit, 0])

        @pl.when(my_y < 2)
        def _():
            wait(grad_parts.at[unit, 0, 0:2], grad_recv.at[unit, 0])

        pulled_send[unit, 1] = jnp.zeros((part, TILE), f32)
        for z in range(1, n_z):

            @pl.when(z > my_z)
            def _():
                with jax.named_scope("s_planeg"):
                    wait(plane_grad_parts.at[unit, z], plane_grad_recv.at[unit, z])
                pulled_send[unit, 1] += plane_grad_parts[unit, z].astype(f32)

        later = pulled_send[unit, 1]
        upper = grad_parts[unit, 0, 2].astype(f32) + grad_parts[unit, 0, 3].astype(f32)
        pulled_half[unit, 0] = (later + upper).astype(half)
        pulled_half[unit, 1] = later.astype(half)
        for step in range(1, Y_SIZE):
            peer = y_peer(step)
            send(
                pulled_half.at[unit, peer // 2],
                pulled.at[part_rows(unit, my_y), :],
                pulled_send_sem.at[unit],
                pulled_recv.at[unit],
                at_y(peer),
            )
        pulled[part_rows(unit, my_y), :] = pulled_half[unit, my_y // 2]

    def send_out(slot, head):
        columns = head_columns(head)
        there = pl.ds(pl.multiple_of(my_head * width + head * TILE, TILE), TILE)
        for step in range(1, n_head):
            peer = lax.rem(my_head + step, n_head)
            send(
                rows_out.at[slot, share_rows(peer), columns],
                outputs[slot].at[:, there],
                out_send.at[slot],
                out_recv.at[slot],
                {"head": peer},
            )
        outputs[slot][:, there] = rows_out[slot, share_rows(my_head), columns]

    def cross(head):
        columns = head_columns(head)
        states = [bucket[bit_index, columns, :] for bit_index in range(ctx_bits)]
        wide, tall = jnp.concatenate(states, axis=1), jnp.concatenate(states, axis=0)
        for row in range(tiles):
            rows = slice(row * TILE, (row + 1) * TILE)
            attended, grad_query = local[0, rows, columns], local[1, rows, columns]
            reads = dot_nn(rows_in[QUERY, rows, columns], wide)
            cot_reads = dot_nt(rows_in[COT, rows, columns], tall)
            for bit_index in range(ctx_bits):
                row_scale = code_column(head, tok_bits + 1 + bit_index, rows)
                at = slice(bit_index * TILE, (bit_index + 1) * TILE)
                attended = attended + row_scale * reads[:, at]
                grad_query = grad_query + row_scale * cot_reads[:, at]
            rows_out[0, rows, columns] = attended.astype(half)
            rows_out[1, rows, columns] = grad_query.astype(half)
        send_out(0, head)
        send_out(1, head)

    def read_buckets(unit):
        for bit_index in range(ctx_bits):
            if bit_index == 0:
                whole = bucket.at[0, unit_range(unit), :]
            elif bit_index == 1:
                whole = bucket.at[1, 0 : 3 * part, :]
            else:
                whole = bucket.at[bit_index, 0 : (Y_SIZE - 1) * part, :]

            @pl.when(jnp.logical_not(is_clear(bit_index)))
            def _():
                with jax.named_scope("s_bucket"):
                    wait(whole, bucket_recv.at[unit, bit_index])

        each_head(unit, cross)

    def pull(head):
        columns = head_columns(head)
        states = (pulled[columns, :].astype(f32) + next_grad[columns, :].astype(f32)).astype(half)
        grad_key = local[2, :, columns] + dot_nt(rows_in[VALUE, :, columns], states)
        rows_out[2, :, columns] = grad_key.astype(half)
        grad_value = local[3, :, columns] + dot_nn(rows_in[KEY, :, columns], states)
        rows_out[3, :, columns] = grad_value.astype(half)
        send_out(2, head)
        send_out(3, head)

    def read_pulled(unit):
        @pl.when(my_y % 2 == 0)
        def _():
            wait(next_grad.at[unit_range(unit), :], next_recv.at[unit])

        with jax.named_scope("s_pulled"):
            wait(pulled.at[0 : (Y_SIZE - 1) * part, :], pulled_recv.at[unit])
        each_head(unit, pull)

    arrived(KEY, 0)
    arrived(VALUE, 0)
    send_state(0)
    arrived(QUERY, 0)
    pl.loop(0, 1)(attend)
    send_plane(0)
    arrived(COT, 0)
    send_grad(0)
    pl.loop(1, 2)(attend)
    send_above(0)
    arrived(KEY, 1)
    arrived(VALUE, 1)
    send_state(1)
    send_plane_grad(0)
    each_head(0, attend_back)
    arrived(QUERY, 1)
    pl.loop(2, 3)(attend)
    send_plane(1)
    arrived(COT, 1)
    send_grad(1)
    read_buckets(0)
    send_pulled(0)
    each_head(0, sum_back)
    pl.loop(3, 4)(attend)
    send_above(1)
    send_plane_grad(1)
    read_pulled(0)
    each_head(1, attend_back)
    read_buckets(1)
    send_pulled(1)
    each_head(1, sum_back)
    read_pulled(1)

    for unit in range(UNITS):
        for slot in range(4):
            wait(
                rows_in.at[slot, 0 : length - share, unit_columns(0, unit)],
                in_send.at[slot, unit],
            )
        wait(state_parts.at[unit, 0 : Y_SIZE - 1], state_send_sem.at[unit])
        for step in range(1, n_z):

            @pl.when(my_z + step < n_z)
            def _():
                wait(pair_send.at[unit, 0], plane_send_sem.at[unit, step])

        @pl.when(my_y % 2 == 0)
        def _():
            wait(bucket.at[0, unit_range(unit), :], bucket_send_sem.at[unit, 0])

        @pl.when(my_y % 2 == 1)
        def _():
            wait(next_grad.at[unit_range(unit), :], next_send_sem.at[unit])

        @pl.when(my_y < 2)
        def _():
            wait(bucket.at[1, 0 : 2 * part, :], bucket_send_sem.at[unit, 1])

        @pl.when(my_y >= 2)
        def _():
            wait(bucket.at[1, 0:part, :], bucket_send_sem.at[unit, 1])
            wait(grad_parts.at[unit, 0, 0 : Y_SIZE - 1], grad_send_sem.at[unit, 0])

        for bit_index in range(z_bits):

            @pl.when(z_bit(bit_index))
            def _():
                three = bucket.at[0, 0 : (Y_SIZE - 1) * part, :]
                wait(three, bucket_send_sem.at[unit, Y_BITS + bit_index])
                wait(three, grad_send_sem.at[unit, 1 + bit_index])
                for block in range(2**bit_index):
                    wait(
                        plane_grad_send.at[unit, bit_index],
                        plane_grad_send_sem.at[unit, 2**bit_index - 1 + block],
                    )

        wait(pulled.at[0 : (Y_SIZE - 1) * part, :], pulled_send_sem.at[unit])

    for slot in range(4):
        sent = rows_out.at[slot, 0 : length - share, :]
        wait(sent, out_send.at[slot])
        with jax.named_scope("s_out"):
            wait(sent, out_recv.at[slot])


def put_out_kernel(*refs):
    held, results, sems = refs[:4], refs[4:8], refs[8]
    copies = [pltpu.make_async_copy(held[i], results[i], sems.at[i]) for i in range(4)]
    for copy in copies:
        copy.start()
    for copy in copies:
        copy.wait()


def put_out(held):
    return pl.pallas_call(
        put_out_kernel,
        out_shape=tuple(jax.ShapeDtypeStruct(array.shape, array.dtype) for array in held),
        in_specs=[pl.BlockSpec(memory_space=pltpu.VMEM)] * 4,
        out_specs=(pl.BlockSpec(memory_space=pl.ANY),) * 4,
        scratch_shapes=[pltpu.SemaphoreType.DMA((4,))],
        name="put_out",
    )(*held)


def on_device(n_ctx, n_head, query_input, key_input, value_input, cotangent, level_codes):
    share, features = query_input.shape
    n_local, n_levels, length = level_codes.shape
    width = features // n_head
    tok_bits = length.bit_length() - 1
    ctx_bits = n_levels - tok_bits - 1
    state_rows = n_local * TILE
    part = state_rows // UNITS // Y_SIZE
    n_z = n_ctx // Y_SIZE
    z_bits = ctx_bits - Y_BITS
    half = jnp.bfloat16
    dma = pltpu.SemaphoreType.DMA
    held = pl.pallas_call(
        functools.partial(kernel, n_ctx, n_head, ctx_bits, tok_bits),
        out_shape=(pltpu.VMEM(query_input.shape, half),) * 4,
        in_specs=[pl.BlockSpec(memory_space=pl.ANY)] * 5,
        out_specs=(pl.BlockSpec(memory_space=pltpu.VMEM),) * 4,
        scratch_shapes=[
            pltpu.VMEM((4, share, features), half),
            pltpu.VMEM((4, length, width), half),
            pltpu.VMEM((n_levels, n_local, length), jnp.int32),
            pltpu.VMEM((TILE, length), jnp.float32),
            pltpu.VMEM((n_local, length, TILE), jnp.float32),
            pltpu.VMEM((TILE, TILE), jnp.int32),
            pltpu.VMEM((n_local, length, length), half),
            pltpu.VMEM((n_local, length, length), half),
            pltpu.VMEM((4, length, width), jnp.float32),
            pltpu.VMEM((4, length, width), half),
            pltpu.VMEM((state_rows, TILE), half),
            pltpu.VMEM((UNITS, Y_SIZE, part, TILE), half),
            pltpu.VMEM((UNITS, 2, part, TILE), half),
            pltpu.VMEM((UNITS, n_z, part, TILE), half),
            pltpu.VMEM((UNITS, z_bits, part, TILE), half),
            pltpu.VMEM((ctx_bits, state_rows, TILE), half),
            pltpu.VMEM((ctx_bits, state_rows, TILE), half),
            pltpu.VMEM((UNITS, ctx_bits - 1, Y_SIZE, part, TILE), half),
            pltpu.VMEM((UNITS, z_bits, part, TILE), half),
            pltpu.VMEM((UNITS, n_z, part, TILE), half),
            pltpu.VMEM((UNITS, 2, part, TILE), jnp.float32),
            pltpu.VMEM((UNITS, 2, part, TILE), half),
            pltpu.VMEM((state_rows, TILE), half),
            pltpu.VMEM((state_rows, TILE), half),
            dma((4,)),
            dma((1,)),
            dma((4, UNITS)),
            dma((4, UNITS)),
            dma((UNITS,)),
            dma((UNITS,)),
            dma((UNITS, n_z)),
            dma((UNITS, n_z)),
            dma((UNITS, ctx_bits)),
            dma((UNITS, ctx_bits)),
            dma((UNITS, ctx_bits - 1)),
            dma((UNITS, ctx_bits - 1)),
            dma((UNITS, n_z)),
            dma((UNITS, n_z)),
            dma((UNITS,)),
            dma((UNITS,)),
            dma((UNITS,)),
            dma((UNITS,)),
            dma((4,)),
            dma((4,)),
        ],
        compiler_params=pltpu.CompilerParams(collective_id=0, has_side_effects=True),
        name="layer",
    )(query_input, key_input, value_input, cotangent, jnp.transpose(level_codes, (1, 0, 2)))
    return put_out([pltpu.with_memory_space_constraint(array, pltpu.VMEM) for array in held])


def solution(mesh):
    rows = P(("ctx", "head"), None)
    return jax.shard_map(
        functools.partial(on_device, mesh.shape["ctx"], mesh.shape["head"]),
        mesh=mesh,
        in_specs=(rows, rows, rows, rows, P("head", None, "ctx")),
        out_specs=(rows, rows, rows, rows),
        check_vma=False,
    )
```

time: 77.8 us -> 64.7 us (0.83)
  Pallas kernels: 77 us -> 64 us
    pallas_call x1, Pallas kernels: 75.7 us -> 62.7 us  [on_device(): pl.pallas_call(functools.partial(kernel, n_ctx, n_head, ctx_bits, tok_bit...]
where the time goes in v3:
time: 64.7 us; the launch traced here: 64.6 us
  Pallas kernels  64 us (99%)
    pallas_call x1, Pallas kernels, on_device(): pl.pallas_call(functools.partial(kernel, n_ctx, n_head, ctx_bits, tok_bit...  62.7 us
    pallas_call x1, Pallas kernels, put_out(): pl.pallas_call(put_out_kernel, out_shape=tuple((jax.ShapeDtypeStruct(arra...  1.35 us

profile of v3, /device:TPU:1, one launch (start us, length us, event | category | flops | bytes accessed | tf_op | source)
XLA Modules:
  0.0 64.6 jit_solution(1172255236798357337)
XLA Ops:
  0.6 62.7 %layer.1 = (bf16[64,4096]{1,0:T(8,128)(2,1)S(1)}, bf16[64,4096]{1,0:T(8,128)(2,1)S(1)}, bf16[64,4096]{1,0:T(8,128)(2,1)S(1)}, bf16[64,4096]{1,0:T(8,128)(2,1)S(1)}) custom-call(bf16[64,4096]{1,0:T(8,128)(2,1)} %query_ref.1, bf16[64,4096]{1,0:T(8,128)(2,1)} %key_ref.1, bf16[64,4096]{1,0:T(8,128)(2,1)} %value_ref.1, bf16[64,4096]{1,0:T(8,128)(2,1)} %cot_ref.1, ...), custom_call_target="tpu_custom_call" | custom-call | tf_op jit(solution)/shard_map/layer/pallas_call | solution.py:655
  63.3 1.3 %put_out.1 = (bf16[64,4096]{1,0:T(8,128)(2,1)}, bf16[64,4096]{1,0:T(8,128)(2,1)}, bf16[64,4096]{1,0:T(8,128)(2,1)}, bf16[64,4096]{1,0:T(8,128)(2,1)}) custom-call(bf16[64,4096]{1,0:T(8,128)(2,1)S(1)} %get-tuple-element.8.refs_0_, bf16[64,4096]{1,0:T(8,128)(2,1)S(1)} %get-tuple-element.9.refs_1_, bf16[64,4096]{1,0:T(8,128)(2,1)S(1)} %get-tuple-element.10.refs_2_, ...), custom_call_target="tpu_custom_call" | custom-call | tf_op jit(solution)/shard_map/put_out/pallas_call | solution.py:633

commit v4 on v3

--- a/solution.py
+++ b/solution.py
@@ -70,6 +70,7 @@
     pulled_half,
     pulled,
     next_grad,
+    answer,
     stage_sem,
     own_sem,
     in_send,
@@ -109,10 +110,13 @@
     part = unit_rows // Y_SIZE
     tiles = length // TILE
     scale = TILE ** (-0.5)
+    byte_count = grad_send.reshape(ctx_bits * n_local * TILE, TILE)
     f32, half = jnp.float32, jnp.bfloat16
 
     def z_bit(bit_index):
         return my_z // 2**bit_index % 2 == 1
+
+    z_count = sum(my_z // 2**bit_index % 2 for bit_index in range(z_bits))
 
     def group_start(bit_index):
         return my_z // 2 ** (bit_index + 1) * 2 ** (bit_index + 1)
@@ -159,8 +163,12 @@
     def greet(device):
         pl.semaphore_signal(barrier, inc=1, device_id=device, device_id_type=MESH)
 
-    for step in range(1, n_z):
-        greet(at_z(lax.rem(my_z + step, n_z)))
+    for z in range(1, n_z):
+
+        @pl.when(z > my_z)
+        def _():
+            greet(at_z(z))
+
     for step in range(1, Y_SIZE):
         greet(at_y(y_peer(step)))
     for step in range(1, n_head):
@@ -170,7 +178,14 @@
     codes_copy = pltpu.make_async_copy(codes_ref, codes, own_sem.at[0])
     codes_copy.start()
     with jax.named_scope("s_barrier"):
-        pl.semaphore_wait(barrier, n_head - 1 + n_z - 1 + Y_SIZE - 1)
+        pl.semaphore_wait(barrier, n_head - 1 + Y_SIZE - 1 + my_z)
+
+    for z in range(n_z):
+
+        @pl.when(z < my_z)
+        def _():
+            pl.semaphore_signal(answer, inc=1, device_id=at_z(z), device_id_type=MESH)
+
 
     for slot, array in enumerate(inputs):
         pltpu.make_async_copy(array, staged.at[slot], stage_sem.at[slot]).wait()
@@ -181,7 +196,7 @@
                 send(
                     staged.at[slot, :, unit_columns(peer, unit)],
                     rows_in.at[slot, share_rows(my_head), unit_columns(0, unit)],
-                    in_send.at[slot, unit],
+                    in_send,
                     in_recv.at[slot, unit],
                     {"head": peer},
                 )
@@ -285,7 +300,7 @@
             send(
                 state_send.at[part_rows(unit, peer), :],
                 state_parts.at[unit, my_y],
-                state_send_sem.at[unit],
+                state_send_sem,
                 state_recv.at[unit],
                 at_y(peer),
             )
@@ -295,7 +310,7 @@
             send(
                 state_send.at[unit_range(unit), :],
                 bucket.at[0, unit_range(unit), :],
-                bucket_send_sem.at[unit, 0],
+                bucket_send_sem.at[0],
                 bucket_recv.at[unit, 0],
                 at_y(my_y + 1),
             )
@@ -309,6 +324,14 @@
         upper = state_parts[unit, 2].astype(f32) + state_parts[unit, 3].astype(f32)
         pair_send[unit, 0] = (lower + upper).astype(half)
         pair_send[unit, 1] = lower.astype(half)
+        if unit == 0:
+
+
+            @pl.when(my_z < n_z - 1)
+            def _():
+                with jax.named_scope("s_answer"):
+                    pl.semaphore_wait(answer, n_z - 1 - my_z)
+
         for step in range(1, n_z):
 
             @pl.when(my_z + step < n_z)
@@ -316,8 +339,8 @@
                 send(
                     pair_send.at[unit, 0],
                     plane_parts.at[unit, my_z],
-                    plane_send_sem.at[unit, step],
-                    plane_recv.at[unit, my_z],
+                    plane_send_sem,
+                    plane_recv.at[unit],
                     at_z(my_z + step),
                 )
 
@@ -328,8 +351,8 @@
                 send(
                     pair_send.at[unit, 1],
                     bucket.at[1, part_rows(unit, my_y), :],
-                    bucket_send_sem.at[unit, 1],
-                    bucket_recv.at[unit, 1],
+                    bucket_send_sem.at[1],
+                    bucket_recv.at[unit, 0],
                     at_y(y),
                 )
 
@@ -338,12 +361,12 @@
                 bucket[1, part_rows(unit, my_y), :] = pair_send[unit, 1]
 
     def send_above(unit):
-        for z in range(n_z - 1):
-
-            @pl.when(z < my_z)
+        for count in range(1, n_z):
+
+            @pl.when(my_z == count)
             def _():
                 with jax.named_scope("s_plane"):
-                    wait(plane_parts.at[unit, z], plane_recv.at[unit, z])
+                    wait(plane_parts.at[unit, 0:count], plane_recv.at[unit])
 
         for bit_index in range(z_bits):
 
@@ -357,8 +380,8 @@
                     send(
                         above_send.at[unit, bit_index],
                         bucket.at[Y_BITS + bit_index, part_rows(unit, my_y), :],
-                        bucket_send_sem.at[unit, Y_BITS + bit_index],
-                        bucket_recv.at[unit, Y_BITS + bit_index],
+                        bucket_send_sem.at[2],
+                        bucket_recv.at[unit, 1],
                         at_y(y_peer(step)),
                     )
                 bucket[Y_BITS + bit_index, part_rows(unit, my_y), :] = above_send[unit, bit_index]
@@ -379,14 +402,14 @@
     def send_grad(unit):
         each_head(unit, grad_of)
 
-        def parts(bit_index):
+        def parts(bit_index, kind):
             for step in range(1, Y_SIZE):
                 peer = y_peer(step)
                 send(
                     grad_send.at[bit_index, part_rows(unit, peer), :],
                     grad_parts.at[unit, bit_index - 1, my_y],
-                    grad_send_sem.at[unit, bit_index - 1],
-                    grad_recv.at[unit, bit_index - 1],
+                    grad_send_sem.at[kind],
+                    grad_recv.at[unit, kind],
                     at_y(peer),
                 )
             grad_parts[unit, bit_index - 1, my_y] = grad_send[bit_index, part_rows(unit, my_y), :]
@@ -395,32 +418,34 @@
 
             @pl.when(z_bit(bit_index))
             def _():
-                parts(Y_BITS + bit_index)
+                parts(Y_BITS + bit_index, 1)
 
         @pl.when(my_y >= 2)
         def _():
-            parts(1)
+            parts(1, 0)
 
         @pl.when(my_y % 2 == 1)
         def _():
             send(
                 grad_send.at[0, unit_range(unit), :],
                 next_grad.at[unit_range(unit), :],
-                next_send_sem.at[unit],
+                next_send_sem,
                 next_recv.at[unit],
                 at_y(my_y - 1),
             )
 
     def send_plane_grad(unit):
+        for count in range(1, z_bits + 1):
+
+            @pl.when(z_count == count)
+            def _():
+                with jax.named_scope("s_grad"):
+                    wait(grad_parts.at[unit, 0:count, 0 : Y_SIZE - 1], grad_recv.at[unit, 1])
+
         for bit_index in range(z_bits):
 
             @pl.when(z_bit(bit_index))
             def _():
-                with jax.named_scope("s_grad"):
-                    wait(
-                        grad_parts.at[unit, 1 + bit_index, 0 : Y_SIZE - 1],
-                        grad_recv.at[unit, 1 + bit_index],
-                    )
                 total = jnp.zeros((part, TILE), f32)
                 for y in range(Y_SIZE):
                     total = total + grad_parts[unit, 1 + bit_index, y].astype(f32)
@@ -429,8 +454,8 @@
                     send(
                         plane_grad_send.at[unit, bit_index],
                         plane_grad_parts.at[unit, my_z],
-                        plane_grad_send_sem.at[unit, 2**bit_index - 1 + block],
-                        plane_grad_recv.at[unit, my_z],
+                        plane_grad_send_sem,
+                        plane_grad_recv.at[unit],
                         at_z(group_start(bit_index) + block),
                     )
 
@@ -443,16 +468,21 @@
         def _():
             wait(grad_parts.at[unit, 0, 0:2], grad_recv.at[unit, 0])
 
-        pulled_send[unit, 1] = jnp.zeros((part, TILE), f32)
+        for count in range(1, n_z):
+
+            @pl.when(n_z - 1 - my_z == count)
+            def _():
+                with jax.named_scope("s_planeg"):
+                    wait(plane_grad_parts.at[unit, 0:count], plane_grad_recv.at[unit])
+
+        pulled_send[...] = jnp.zeros_like(pulled_send)
         for z in range(1, n_z):
 
             @pl.when(z > my_z)
             def _():
-                with jax.named_scope("s_planeg"):
-                    wait(plane_grad_parts.at[unit, z], plane_grad_recv.at[unit, z])
-                pulled_send[unit, 1] += plane_grad_parts[unit, z].astype(f32)
-
-        later = pulled_send[unit, 1]
+                pulled_send[...] += plane_grad_parts[unit, z].astype(f32)
+
+        later = pulled_send[...]
         upper = grad_parts[unit, 0, 2].astype(f32) + grad_parts[unit, 0, 3].astype(f32)
         pulled_half[unit, 0] = (later + upper).astype(half)
         pulled_half[unit, 1] = later.astype(half)
@@ -461,7 +491,7 @@
             send(
                 pulled_half.at[unit, peer // 2],
                 pulled.at[part_rows(unit, my_y), :],
-                pulled_send_sem.at[unit],
+                pulled_send_sem,
                 pulled_recv.at[unit],
                 at_y(peer),
             )
@@ -475,8 +505,8 @@
             send(
                 rows_out.at[slot, share_rows(peer), columns],
                 outputs[slot].at[:, there],
-                out_send.at[slot],
-                out_recv.at[slot],
+                out_send,
+                out_recv,
                 {"head": peer},
             )
         outputs[slot][:, there] = rows_out[slot, share_rows(my_head), columns]
@@ -501,18 +531,21 @@
         send_out(1, head)
 
     def read_buckets(unit):
-        for bit_index in range(ctx_bits):
-            if bit_index == 0:
-                whole = bucket.at[0, unit_range(unit), :]
-            elif bit_index == 1:
-                whole = bucket.at[1, 0 : 3 * part, :]
-            else:
-                whole = bucket.at[bit_index, 0 : (Y_SIZE - 1) * part, :]
-
-            @pl.when(jnp.logical_not(is_clear(bit_index)))
+        for y, count in ((1, Y_SIZE), (2, Y_SIZE - 1), (3, 2 * Y_SIZE - 1)):
+
+            @pl.when(my_y == y)
             def _():
                 with jax.named_scope("s_bucket"):
-                    wait(whole, bucket_recv.at[unit, bit_index])
+                    wait(byte_count.at[0 : count * part, :], bucket_recv.at[unit, 0])
+
+        for count in range(1, z_bits + 1):
+
+            @pl.when(z_count == count)
+            def _():
+                with jax.named_scope("s_bucketz"):
+                    wait(
+                        byte_count.at[0 : count * (Y_SIZE - 1) * part, :], bucket_recv.at[unit, 1]
+                    )
 
         each_head(unit, cross)
 
@@ -545,17 +578,17 @@
     send_grad(0)
     pl.loop(1, 2)(attend)
     send_above(0)
+    each_head(0, attend_back)
     arrived(KEY, 1)
     arrived(VALUE, 1)
     send_state(1)
     send_plane_grad(0)
-    each_head(0, attend_back)
+    read_buckets(0)
     arrived(QUERY, 1)
     pl.loop(2, 3)(attend)
     send_plane(1)
     arrived(COT, 1)
     send_grad(1)
-    read_buckets(0)
     send_pulled(0)
     each_head(0, sum_back)
     pl.loop(3, 4)(attend)
@@ -568,56 +601,50 @@
     each_head(1, sum_back)
     read_pulled(1)
 
-    for unit in range(UNITS):
-        for slot in range(4):
-            wait(
-                rows_in.at[slot, 0 : length - share, unit_columns(0, unit)],
-                in_send.at[slot, unit],
-            )
-        wait(state_parts.at[unit, 0 : Y_SIZE - 1], state_send_sem.at[unit])
-        for step in range(1, n_z):
-
-            @pl.when(my_z + step < n_z)
-            def _():
-                wait(pair_send.at[unit, 0], plane_send_sem.at[unit, step])
-
-        @pl.when(my_y % 2 == 0)
-        def _():
-            wait(bucket.at[0, unit_range(unit), :], bucket_send_sem.at[unit, 0])
-
-        @pl.when(my_y % 2 == 1)
-        def _():
-            wait(next_grad.at[unit_range(unit), :], next_send_sem.at[unit])
-
-        @pl.when(my_y < 2)
-        def _():
-            wait(bucket.at[1, 0 : 2 * part, :], bucket_send_sem.at[unit, 1])
-
-        @pl.when(my_y >= 2)
-        def _():
-            wait(bucket.at[1, 0:part, :], bucket_send_sem.at[unit, 1])
-            wait(grad_parts.at[unit, 0, 0 : Y_SIZE - 1], grad_send_sem.at[unit, 0])
-
-        for bit_index in range(z_bits):
-
-            @pl.when(z_bit(bit_index))
-            def _():
-                three = bucket.at[0, 0 : (Y_SIZE - 1) * part, :]
-                wait(three, bucket_send_sem.at[unit, Y_BITS + bit_index])
-                wait(three, grad_send_sem.at[unit, 1 + bit_index])
-                for block in range(2**bit_index):
-                    wait(
-                        plane_grad_send.at[unit, bit_index],
-                        plane_grad_send_sem.at[unit, 2**bit_index - 1 + block],
-                    )
-
-        wait(pulled.at[0 : (Y_SIZE - 1) * part, :], pulled_send_sem.at[unit])
-
-    for slot in range(4):
-        sent = rows_out.at[slot, 0 : length - share, :]
-        wait(sent, out_send.at[slot])
-        with jax.named_scope("s_out"):
-            wait(sent, out_recv.at[slot])
+    def sent(count, sem):
+        wait(byte_count.at[0 : count * UNITS * part, :], sem)
+
+    wait(rows_in.at[:, 0 : length - share, :], in_send)
+    sent(Y_SIZE - 1, state_send_sem)
+    sent(Y_SIZE - 1, pulled_send_sem)
+
+    @pl.when(my_y % 2 == 0)
+    def _():
+        sent(Y_SIZE, bucket_send_sem.at[0])
+
+    @pl.when(my_y % 2 == 1)
+    def _():
+        sent(Y_SIZE, next_send_sem)
+
+    @pl.when(my_y < 2)
+    def _():
+        sent(2, bucket_send_sem.at[1])
+
+    @pl.when(my_y >= 2)
+    def _():
+        sent(1, bucket_send_sem.at[1])
+        sent(Y_SIZE - 1, grad_send_sem.at[0])
+
+    for count in range(1, z_bits + 1):
+
+        @pl.when(z_count == count)
+        def _():
+            sent(count * (Y_SIZE - 1), bucket_send_sem.at[2])
+            sent(count * (Y_SIZE - 1), grad_send_sem.at[1])
+
+    for count in range(1, n_z):
+
+        @pl.when(my_z == count)
+        def _():
+            sent(count, plane_grad_send_sem)
+
+        @pl.when(n_z - 1 - my_z == count)
+        def _():
+            sent(count, plane_send_sem)
+
+    wait(rows_out.at[:, 0 : length - share, :], out_send)
+    with jax.named_scope("s_out"):
+        wait(rows_out.at[:, 0 : length - share, :], out_recv)
 
 
 def put_out_kernel(*refs):
@@ -678,30 +705,31 @@
             pltpu.VMEM((UNITS, ctx_bits - 1, Y_SIZE, part, TILE), half),
             pltpu.VMEM((UNITS, z_bits, part, TILE), half),
             pltpu.VMEM((UNITS, n_z, part, TILE), half),
-            pltpu.VMEM((UNITS, 2, part, TILE), jnp.float32),
+            pltpu.VMEM((part, TILE), jnp.float32),
             pltpu.VMEM((UNITS, 2, part, TILE), half),
             pltpu.VMEM((state_rows, TILE), half),
             pltpu.VMEM((state_rows, TILE), half),
+            pltpu.SemaphoreType.REGULAR,
             dma((4,)),
             dma((1,)),
+            dma,
             dma((4, UNITS)),
-            dma((4, UNITS)),
+            dma,
             dma((UNITS,)),
+            dma,
             dma((UNITS,)),
-            dma((UNITS, n_z)),
-            dma((UNITS, n_z)),
-            dma((UNITS, ctx_bits)),
-            dma((UNITS, ctx_bits)),
-            dma((UNITS, ctx_bits - 1)),
-            dma((UNITS, ctx_bits - 1)),
-            dma((UNITS, n_z)),
-            dma((UNITS, n_z)),
+            dma((3,)),
+            dma((UNITS, 2)),
+            dma((2,)),
+            dma((UNITS, 2)),
+            dma,
             dma((UNITS,)),
+            dma,
             dma((UNITS,)),
+            dma,
             dma((UNITS,)),
-            dma((UNITS,)),
-            dma((4,)),
-            dma((4,)),
+            dma,
+            dma,
         ],
         compiler_params=pltpu.CompilerParams(collective_id=0, has_side_effects=True),
         name="layer",

time: 64.7 us -> 60.7 us (0.938); the launches traced: 64.6 us -> 59.6 us
  Pallas kernels: 64 us -> 59 us
    pallas_call x1, Pallas kernels: 62.7 us -> 57.6 us  [on_device(): pl.pallas_call(functools.partial(kernel, n_ctx, n_head, ctx_bits, tok_bit...]
where the time goes in v4:
time: 60.7 us; the launch traced here: 59.6 us
  Pallas kernels  59 us (97%)
  between operations  0.64 us (1%)
    pallas_call x1, Pallas kernels, on_device(): pl.pallas_call(functools.partial(kernel, n_ctx, n_head, ctx_bits, tok_bit...  57.6 us
    pallas_call x1, Pallas kernels, put_out(): pl.pallas_call(put_out_kernel, out_shape=tuple((jax.ShapeDtypeStruct(arra...  1.35 us

profile of v4, /device:TPU:1, one launch (start us, length us, event | category | flops | bytes accessed | tf_op | source)
XLA Modules:
  0.0 59.6 jit_solution(7673867590009468910)
XLA Ops:
  0.6 57.6 %layer.1 = (bf16[64,4096]{1,0:T(8,128)(2,1)S(1)}, bf16[64,4096]{1,0:T(8,128)(2,1)S(1)}, bf16[64,4096]{1,0:T(8,128)(2,1)S(1)}, bf16[64,4096]{1,0:T(8,128)(2,1)S(1)}) custom-call(bf16[64,4096]{1,0:T(8,128)(2,1)} %query_ref.1, bf16[64,4096]{1,0:T(8,128)(2,1)} %key_ref.1, bf16[64,4096]{1,0:T(8,128)(2,1)} %value_ref.1, bf16[64,4096]{1,0:T(8,128)(2,1)} %cot_ref.1, ...), custom_call_target="tpu_custom_call" | custom-call | tf_op jit(solution)/shard_map/layer/pallas_call | solution.py:682
  58.3 1.3 %put_out.1 = (bf16[64,4096]{1,0:T(8,128)(2,1)}, bf16[64,4096]{1,0:T(8,128)(2,1)}, bf16[64,4096]{1,0:T(8,128)(2,1)}, bf16[64,4096]{1,0:T(8,128)(2,1)}) custom-call(bf16[64,4096]{1,0:T(8,128)(2,1)S(1)} %get-tuple-element.8.refs_0_, bf16[64,4096]{1,0:T(8,128)(2,1)S(1)} %get-tuple-element.9.refs_1_, bf16[64,4096]{1,0:T(8,128)(2,1)S(1)} %get-tuple-element.10.refs_2_, ...), custom_call_target="tpu_custom_call" | custom-call | tf_op jit(solution)/shard_map/put_out/pallas_call | solution.py:660

commit v5 on v4

--- a/solution.py
+++ b/solution.py
@@ -10,7 +10,7 @@
 MESH = pl.DeviceIdType.MESH
 KEY, VALUE, QUERY, COT = range(4)
 TILE = 128
-UNITS = 2
+UNITS = 4
 Y_SIZE, Y_BITS = 4, 2
 
 
@@ -568,38 +568,41 @@
             wait(pulled.at[0 : (Y_SIZE - 1) * part, :], pulled_recv.at[unit])
         each_head(unit, pull)
 
-    arrived(KEY, 0)
-    arrived(VALUE, 0)
-    send_state(0)
-    arrived(QUERY, 0)
-    pl.loop(0, 1)(attend)
-    send_plane(0)
-    arrived(COT, 0)
-    send_grad(0)
-    pl.loop(1, 2)(attend)
-    send_above(0)
-    each_head(0, attend_back)
-    arrived(KEY, 1)
-    arrived(VALUE, 1)
-    send_state(1)
-    send_plane_grad(0)
-    read_buckets(0)
-    arrived(QUERY, 1)
-    pl.loop(2, 3)(attend)
-    send_plane(1)
-    arrived(COT, 1)
-    send_grad(1)
-    send_pulled(0)
-    each_head(0, sum_back)
-    pl.loop(3, 4)(attend)
-    send_above(1)
-    send_plane_grad(1)
-    read_pulled(0)
-    each_head(1, attend_back)
-    read_buckets(1)
-    send_pulled(1)
-    each_head(1, sum_back)
-    read_pulled(1)
+    def step_in(unit):
+        arrived(KEY, unit)
+        arrived(VALUE, unit)
+        send_state(unit)
+        if unit >= 2:
+            read_buckets(unit - 2)
+        arrived(QUERY, unit)
+        each_head(unit, attend)
+        if unit >= 1:
+            send_plane_grad(unit - 1)
+            send_above(unit - 1)
+        if unit >= 3:
+            read_pulled(unit - 3)
+        arrived(COT, unit)
+        send_grad(unit)
+        send_plane(unit)
+        if unit >= 2:
+            send_pulled(unit - 2)
+        each_head(unit, attend_back)
+        if unit >= 1:
+            each_head(unit - 1, sum_back)
+
+    for unit in range(UNITS):
+        step_in(unit)
+    last = UNITS - 1
+    read_buckets(last - 1)
+    send_plane_grad(last)
+    send_above(last)
+    read_pulled(last - 2)
+    send_pulled(last - 1)
+    each_head(last, sum_back)
+    read_buckets(last)
+    read_pulled(last - 1)
+    send_pulled(last)
+    read_pulled(last)
 
     def sent(count, sem):
         wait(byte_count.at[0 : count * UNITS * part, :], sem)

time: 60.7 us -> 55.5 us (0.914); the launches traced: 59.6 us -> 55.4 us
  Pallas kernels: 59 us -> 54.6 us
    pallas_call x1, Pallas kernels: 57.6 us -> 53.2 us  [on_device(): pl.pallas_call(functools.partial(kernel, n_ctx, n_head, ctx_bits, tok_bit...]
where the time goes in v5:
time: 55.5 us; the launch traced here: 55.4 us
  Pallas kernels  54.6 us (98%)
  between operations  0.8 us (1%)
    pallas_call x1, Pallas kernels, on_device(): pl.pallas_call(functools.partial(kernel, n_ctx, n_head, ctx_bits, tok_bit...  53.2 us
    pallas_call x1, Pallas kernels, put_out(): pl.pallas_call(put_out_kernel, out_shape=tuple((jax.ShapeDtypeStruct(arra...  1.35 us

profile of v5, /device:TPU:1, one launch (start us, length us, event | category | flops | bytes accessed | tf_op | source)
XLA Modules:
  0.0 55.4 jit_solution(4393312658575150608)
XLA Ops:
  0.6 53.2 %layer.1 = (bf16[64,4096]{1,0:T(8,128)(2,1)S(1)}, bf16[64,4096]{1,0:T(8,128)(2,1)S(1)}, bf16[64,4096]{1,0:T(8,128)(2,1)S(1)}, bf16[64,4096]{1,0:T(8,128)(2,1)S(1)}) custom-call(bf16[64,4096]{1,0:T(8,128)(2,1)} %query_ref.1, bf16[64,4096]{1,0:T(8,128)(2,1)} %key_ref.1, bf16[64,4096]{1,0:T(8,128)(2,1)} %value_ref.1, bf16[64,4096]{1,0:T(8,128)(2,1)} %cot_ref.1, ...), custom_call_target="tpu_custom_call" | custom-call | tf_op jit(solution)/shard_map/layer/pallas_call | solution.py:685
  53.9 1.3 %put_out.1 = (bf16[64,4096]{1,0:T(8,128)(2,1)}, bf16[64,4096]{1,0:T(8,128)(2,1)}, bf16[64,4096]{1,0:T(8,128)(2,1)}, bf16[64,4096]{1,0:T(8,128)(2,1)}) custom-call(bf16[64,4096]{1,0:T(8,128)(2,1)S(1)} %get-tuple-element.8.refs_0_, bf16[64,4096]{1,0:T(8,128)(2,1)S(1)} %get-tuple-element.9.refs_1_, bf16[64,4096]{1,0:T(8,128)(2,1)S(1)} %get-tuple-element.10.refs_2_, ...), custom_call_target="tpu_custom_call" | custom-call | tf_op jit(solution)/shard_map/put_out/pallas_call | solution.py:663

commit v6 on v5

--- a/solution.py
+++ b/solution.py
@@ -73,23 +73,16 @@
     answer,
     stage_sem,
     own_sem,
-    in_send,
+    x_send,
+    ctx_send,
     in_recv,
-    state_send_sem,
     state_recv,
-    plane_send_sem,
     plane_recv,
-    bucket_send_sem,
     bucket_recv,
-    grad_send_sem,
     grad_recv,
-    plane_grad_send_sem,
     plane_grad_recv,
-    pulled_send_sem,
     pulled_recv,
-    next_send_sem,
     next_recv,
-    out_send,
     out_recv,
 ):
     my_ctx = lax.axis_index("ctx")
@@ -169,8 +162,12 @@
         def _():
             greet(at_z(z))
 
-    for step in range(1, Y_SIZE):
-        greet(at_y(y_peer(step)))
+    for y in range(1, Y_SIZE):
+
+        @pl.when(y > my_y)
+        def _():
+            greet(at_y(y))
+
     for step in range(1, n_head):
         greet({"head": lax.rem(my_head + step, n_head)})
     for slot, array in enumerate(inputs):
@@ -178,13 +175,19 @@
     codes_copy = pltpu.make_async_copy(codes_ref, codes, own_sem.at[0])
     codes_copy.start()
     with jax.named_scope("s_barrier"):
-        pl.semaphore_wait(barrier, n_head - 1 + Y_SIZE - 1 + my_z)
-
-    for z in range(n_z):
+        pl.semaphore_wait(barrier, n_head - 1 + my_y + my_z)
+
+    for y in range(Y_SIZE - 1):
+
+        @pl.when(y < my_y)
+        def _():
+            pl.semaphore_signal(answer.at[0], inc=1, device_id=at_y(y), device_id_type=MESH)
+
+    for z in range(n_z - 1):
 
         @pl.when(z < my_z)
         def _():
-            pl.semaphore_signal(answer, inc=1, device_id=at_z(z), device_id_type=MESH)
+            pl.semaphore_signal(answer.at[1], inc=1, device_id=at_z(z), device_id_type=MESH)
 
 
     for slot, array in enumerate(inputs):
@@ -196,8 +199,8 @@
                 send(
                     staged.at[slot, :, unit_columns(peer, unit)],
                     rows_in.at[slot, share_rows(my_head), unit_columns(0, unit)],
-                    in_send,
-                    in_recv.at[slot, unit],
+                    x_send,
+                    in_recv.at[max(slot - 1, 0), unit],
                     {"head": peer},
                 )
 
@@ -231,10 +234,10 @@
     def _():
         next_grad[...] = jnp.zeros_like(next_grad)
 
-    def arrived(slot, unit):
-        others = rows_in.at[slot, 0 : length - share, unit_columns(0, unit)]
+    def arrived(slots, unit):
+        others = rows_in.at[slots, 0 : length - share, unit_columns(0, unit)]
         with jax.named_scope("s_in"):
-            wait(others, in_recv.at[slot, unit])
+            wait(others, in_recv.at[max(slots.stop - 2, 0), unit])
 
     def code_column(head, level_index, rows):
         return code_cols[head, rows, level_index : level_index + 1] * (
@@ -295,12 +298,19 @@
 
     def send_state(unit):
         each_head(unit, state_of)
+        if unit == 0:
+
+            @pl.when(my_y < Y_SIZE - 1)
+            def _():
+                with jax.named_scope("s_answery"):
+                    pl.semaphore_wait(answer.at[0], Y_SIZE - 1 - my_y)
+
         for step in range(1, Y_SIZE):
             peer = y_peer(step)
             send(
                 state_send.at[part_rows(unit, peer), :],
                 state_parts.at[unit, my_y],
-                state_send_sem,
+                ctx_send,
                 state_recv.at[unit],
                 at_y(peer),
             )
@@ -310,7 +320,7 @@
             send(
                 state_send.at[unit_range(unit), :],
                 bucket.at[0, unit_range(unit), :],
-                bucket_send_sem.at[0],
+                ctx_send,
                 bucket_recv.at[unit, 0],
                 at_y(my_y + 1),
             )
@@ -330,7 +340,7 @@
             @pl.when(my_z < n_z - 1)
             def _():
                 with jax.named_scope("s_answer"):
-                    pl.semaphore_wait(answer, n_z - 1 - my_z)
+                    pl.semaphore_wait(answer.at[1], n_z - 1 - my_z)
 
         for step in range(1, n_z):
 
@@ -339,7 +349,7 @@
                 send(
                     pair_send.at[unit, 0],
                     plane_parts.at[unit, my_z],
-                    plane_send_sem,
+                    ctx_send,
                     plane_recv.at[unit],
                     at_z(my_z + step),
                 )
@@ -351,7 +361,7 @@
                 send(
                     pair_send.at[unit, 1],
                     bucket.at[1, part_rows(unit, my_y), :],
-                    bucket_send_sem.at[1],
+                    ctx_send,
                     bucket_recv.at[unit, 0],
                     at_y(y),
                 )
@@ -380,7 +390,7 @@
                     send(
                         above_send.at[unit, bit_index],
                         bucket.at[Y_BITS + bit_index, part_rows(unit, my_y), :],
-                        bucket_send_sem.at[2],
+                        ctx_send,
                         bucket_recv.at[unit, 1],
                         at_y(y_peer(step)),
                     )
@@ -408,7 +418,7 @@
                 send(
                     grad_send.at[bit_index, part_rows(unit, peer), :],
                     grad_parts.at[unit, bit_index - 1, my_y],
-                    grad_send_sem.at[kind],
+                    ctx_send,
                     grad_recv.at[unit, kind],
                     at_y(peer),
                 )
@@ -429,7 +439,7 @@
             send(
                 grad_send.at[0, unit_range(unit), :],
                 next_grad.at[unit_range(unit), :],
-                next_send_sem,
+                ctx_send,
                 next_recv.at[unit],
                 at_y(my_y - 1),
             )
@@ -454,7 +464,7 @@
                     send(
                         plane_grad_send.at[unit, bit_index],
                         plane_grad_parts.at[unit, my_z],
-                        plane_grad_send_sem,
+                        ctx_send,
                         plane_grad_recv.at[unit],
                         at_z(group_start(bit_index) + block),
                     )
@@ -491,7 +501,7 @@
             send(
                 pulled_half.at[unit, peer // 2],
                 pulled.at[part_rows(unit, my_y), :],
-                pulled_send_sem,
+                ctx_send,
                 pulled_recv.at[unit],
                 at_y(peer),
             )
@@ -505,7 +515,7 @@
             send(
                 rows_out.at[slot, share_rows(peer), columns],
                 outputs[slot].at[:, there],
-                out_send,
+                x_send,
                 out_recv,
                 {"head": peer},
             )
@@ -569,19 +579,18 @@
         each_head(unit, pull)
 
     def step_in(unit):
-        arrived(KEY, unit)
-        arrived(VALUE, unit)
+        arrived(slice(KEY, VALUE + 1), unit)
         send_state(unit)
         if unit >= 2:
             read_buckets(unit - 2)
-        arrived(QUERY, unit)
+        arrived(slice(QUERY, QUERY + 1), unit)
         each_head(unit, attend)
         if unit >= 1:
             send_plane_grad(unit - 1)
             send_above(unit - 1)
         if unit >= 3:
             read_pulled(unit - 3)
-        arrived(COT, unit)
+        arrived(slice(COT, COT + 1), unit)
         send_grad(unit)
         send_plane(unit)
         if unit >= 2:
@@ -604,48 +613,18 @@
     send_pulled(last)
     read_pulled(last)
 
-    def sent(count, sem):
-        wait(byte_count.at[0 : count * UNITS * part, :], sem)
-
-    wait(rows_in.at[:, 0 : length - share, :], in_send)
-    sent(Y_SIZE - 1, state_send_sem)
-    sent(Y_SIZE - 1, pulled_send_sem)
-
-    @pl.when(my_y % 2 == 0)
-    def _():
-        sent(Y_SIZE, bucket_send_sem.at[0])
-
-    @pl.when(my_y % 2 == 1)
-    def _():
-        sent(Y_SIZE, next_send_sem)
-
-    @pl.when(my_y < 2)
-    def _():
-        sent(2, bucket_send_sem.at[1])
-
-    @pl.when(my_y >= 2)
-    def _():
-        sent(1, bucket_send_sem.at[1])
-        sent(Y_SIZE - 1, grad_send_sem.at[0])
-
-    for count in range(1, z_bits + 1):
-
-        @pl.when(z_count == count)
-        def _():
-            sent(count * (Y_SIZE - 1), bucket_send_sem.at[2])
-            sent(count * (Y_SIZE - 1), grad_send_sem.at[1])
-
-    for count in range(1, n_z):
-
-        @pl.when(my_z == count)
-        def _():
-            sent(count, plane_grad_send_sem)
-
-        @pl.when(n_z - 1 - my_z == count)
-        def _():
-            sent(count, plane_send_sem)
-
-    wait(rows_out.at[:, 0 : length - share, :], out_send)
+    flat = local.reshape(local.shape[0] * length, width)
+    part_bytes = UNITS * part * TILE * 2 // (width * 4)
+    for low in (True, False):
+        for count in range(z_bits + 1):
+
+            @pl.when(((my_y < 2) == low) & (z_count == count))
+            def _():
+                parts = 2 * (Y_SIZE - 1) + Y_SIZE + n_z - 1
+                parts += (2 if low else 4) + 2 * (Y_SIZE - 1) * count
+                wait(flat.at[0 : parts * part_bytes, :], ctx_send)
+
+    wait(local.at[:, 0 : length - share, :], x_send)
     with jax.named_scope("s_out"):
         wait(rows_out.at[:, 0 : length - share, :], out_recv)
 
@@ -712,26 +691,19 @@
             pltpu.VMEM((UNITS, 2, part, TILE), half),
             pltpu.VMEM((state_rows, TILE), half),
             pltpu.VMEM((state_rows, TILE), half),
-            pltpu.SemaphoreType.REGULAR,
+            pltpu.SemaphoreType.REGULAR((2,)),
             dma((4,)),
             dma((1,)),
             dma,
-            dma((4, UNITS)),
             dma,
+            dma((3, UNITS)),
             dma((UNITS,)),
-            dma,
             dma((UNITS,)),
-            dma((3,)),
             dma((UNITS, 2)),
-            dma((2,)),
             dma((UNITS, 2)),
-            dma,
             dma((UNITS,)),
-            dma,
             dma((UNITS,)),
-            dma,
             dma((UNITS,)),
-            dma,
             dma,
         ],
         compiler_params=pltpu.CompilerParams(collective_id=0, has_side_effects=True),

time: 55.5 us -> 55.2 us (level)
  no operation moved by 1% of the time
where the time goes in v6:
time: 55.2 us; the launch traced here: 55.1 us
  Pallas kernels  54.3 us (98%)
  between operations  0.8 us (1%)
    pallas_call x1, Pallas kernels, on_device(): pl.pallas_call(functools.partial(kernel, n_ctx, n_head, ctx_bits, tok_bit...  52.9 us
    pallas_call x1, Pallas kernels, put_out(): pl.pallas_call(put_out_kernel, out_shape=tuple((jax.ShapeDtypeStruct(arra...  1.35 us

profile of v6, /device:TPU:1, one launch (start us, length us, event | category | flops | bytes accessed | tf_op | source)
XLA Modules:
  0.0 55.1 jit_solution(7086076138821061301)
XLA Ops:
  0.6 52.9 %layer.1 = (bf16[64,4096]{1,0:T(8,128)(2,1)S(1)}, bf16[64,4096]{1,0:T(8,128)(2,1)S(1)}, bf16[64,4096]{1,0:T(8,128)(2,1)S(1)}, bf16[64,4096]{1,0:T(8,128)(2,1)S(1)}) custom-call(bf16[64,4096]{1,0:T(8,128)(2,1)} %query_ref.1, bf16[64,4096]{1,0:T(8,128)(2,1)} %key_ref.1, bf16[64,4096]{1,0:T(8,128)(2,1)} %value_ref.1, bf16[64,4096]{1,0:T(8,128)(2,1)} %cot_ref.1, ...), custom_call_target="tpu_custom_call" | custom-call | tf_op jit(solution)/shard_map/layer/pallas_call | solution.py:664
  53.5 1.3 %put_out.1 = (bf16[64,4096]{1,0:T(8,128)(2,1)}, bf16[64,4096]{1,0:T(8,128)(2,1)}, bf16[64,4096]{1,0:T(8,128)(2,1)}, bf16[64,4096]{1,0:T(8,128)(2,1)}) custom-call(bf16[64,4096]{1,0:T(8,128)(2,1)S(1)} %get-tuple-element.8.refs_0_, bf16[64,4096]{1,0:T(8,128)(2,1)S(1)} %get-tuple-element.9.refs_1_, bf16[64,4096]{1,0:T(8,128)(2,1)S(1)} %get-tuple-element.10.refs_2_, ...), custom_call_target="tpu_custom_call" | custom-call | tf_op jit(solution)/shard_map/put_out/pallas_call | solution.py:642

commit v7 on v6

--- a/solution.py
+++ b/solution.py
@@ -117,6 +117,15 @@
     def y_peer(step):
         return lax.rem(my_y + step, Y_SIZE)
 
+    chips = n_head // 2
+    far = chips // 2
+    near = [step for reach in range(far - 1, 0, -1) for step in (reach, chips - reach)]
+    line = [
+        lax.rem(my_head // 2 + step, chips) * 2 + lax.rem(my_head + core, 2)
+        for step, core in [(far, 0), (far, 1)] + [(step, core) for core in (0, 1) for step in near]
+        if step
+    ] + [my_head // 2 * 2 + lax.rem(my_head + 1, 2)]
+
     def at_y(y):
         return {"ctx": my_z * Y_SIZE + y}
 
@@ -194,8 +203,7 @@
         pltpu.make_async_copy(array, staged.at[slot], stage_sem.at[slot]).wait()
     for unit in range(UNITS):
         for slot in range(4):
-            for step in range(1, n_head):
-                peer = lax.rem(my_head + step, n_head)
+            for peer in line:
                 send(
                     staged.at[slot, :, unit_columns(peer, unit)],
                     rows_in.at[slot, share_rows(my_head), unit_columns(0, unit)],
@@ -510,8 +518,7 @@
     def send_out(slot, head):
         columns = head_columns(head)
         there = pl.ds(pl.multiple_of(my_head * width + head * TILE, TILE), TILE)
-        for step in range(1, n_head):
-            peer = lax.rem(my_head + step, n_head)
+        for peer in line:
             send(
                 rows_out.at[slot, share_rows(peer), columns],
                 outputs[slot].at[:, there],

time: 55.2 us -> 54.9 us (level)
  no operation moved by 1% of the time
where the time goes in v7:
time: 54.9 us; the launch traced here: 54.8 us
  Pallas kernels  54 us (98%)
  between operations  0.8 us (1%)
    pallas_call x1, Pallas kernels, on_device(): pl.pallas_call(functools.partial(kernel, n_ctx, n_head, ctx_bits, tok_bit...  52.6 us
    pallas_call x1, Pallas kernels, put_out(): pl.pallas_call(put_out_kernel, out_shape=tuple((jax.ShapeDtypeStruct(arra...  1.35 us

profile of v7, /device:TPU:1, one launch (start us, length us, event | category | flops | bytes accessed | tf_op | source)
XLA Modules:
  0.0 54.8 jit_solution(12089354297004898467)
XLA Ops:
  0.6 52.6 %layer.1 = (bf16[64,4096]{1,0:T(8,128)(2,1)S(1)}, bf16[64,4096]{1,0:T(8,128)(2,1)S(1)}, bf16[64,4096]{1,0:T(8,128)(2,1)S(1)}, bf16[64,4096]{1,0:T(8,128)(2,1)S(1)}) custom-call(bf16[64,4096]{1,0:T(8,128)(2,1)} %query_ref.1, bf16[64,4096]{1,0:T(8,128)(2,1)} %key_ref.1, bf16[64,4096]{1,0:T(8,128)(2,1)} %value_ref.1, bf16[64,4096]{1,0:T(8,128)(2,1)} %cot_ref.1, ...), custom_call_target="tpu_custom_call" | custom-call | tf_op jit(solution)/shard_map/layer/pallas_call | solution.py:671
  53.3 1.3 %put_out.1 = (bf16[64,4096]{1,0:T(8,128)(2,1)}, bf16[64,4096]{1,0:T(8,128)(2,1)}, bf16[64,4096]{1,0:T(8,128)(2,1)}, bf16[64,4096]{1,0:T(8,128)(2,1)}) custom-call(bf16[64,4096]{1,0:T(8,128)(2,1)S(1)} %get-tuple-element.8.refs_0_, bf16[64,4096]{1,0:T(8,128)(2,1)S(1)} %get-tuple-element.9.refs_1_, bf16[64,4096]{1,0:T(8,128)(2,1)S(1)} %get-tuple-element.10.refs_2_, ...), custom_call_target="tpu_custom_call" | custom-call | tf_op jit(solution)/shard_map/put_out/pallas_call | solution.py:649

commit v8 on v7

--- a/solution.py
+++ b/solution.py
@@ -115,7 +115,7 @@
         return my_z // 2 ** (bit_index + 1) * 2 ** (bit_index + 1)
 
     def y_peer(step):
-        return lax.rem(my_y + step, Y_SIZE)
+        return lax.rem(my_y + (2, 1, 3)[step - 1], Y_SIZE)
 
     chips = n_head // 2
     far = chips // 2

time: 54.9 us -> 54.9 us (level)
  no operation moved by 1% of the time
where the time goes in v8:
time: 54.9 us; the launch traced here: 54.8 us
  Pallas kernels  54 us (98%)
  between operations  0.8 us (1%)
    pallas_call x1, Pallas kernels, on_device(): pl.pallas_call(functools.partial(kernel, n_ctx, n_head, ctx_bits, tok_bit...  52.6 us
    pallas_call x1, Pallas kernels, put_out(): pl.pallas_call(put_out_kernel, out_shape=tuple((jax.ShapeDtypeStruct(arra...  1.35 us

profile of v8, /device:TPU:1, one launch (start us, length us, event | category | flops | bytes accessed | tf_op | source)
XLA Modules:
  0.0 54.8 jit_solution(15612131539444224525)
XLA Ops:
  0.6 52.6 %layer.1 = (bf16[64,4096]{1,0:T(8,128)(2,1)S(1)}, bf16[64,4096]{1,0:T(8,128)(2,1)S(1)}, bf16[64,4096]{1,0:T(8,128)(2,1)S(1)}, bf16[64,4096]{1,0:T(8,128)(2,1)S(1)}) custom-call(bf16[64,4096]{1,0:T(8,128)(2,1)} %query_ref.1, bf16[64,4096]{1,0:T(8,128)(2,1)} %key_ref.1, bf16[64,4096]{1,0:T(8,128)(2,1)} %value_ref.1, bf16[64,4096]{1,0:T(8,128)(2,1)} %cot_ref.1, ...), custom_call_target="tpu_custom_call" | custom-call | tf_op jit(solution)/shard_map/layer/pallas_call | solution.py:671
  53.3 1.3 %put_out.1 = (bf16[64,4096]{1,0:T(8,128)(2,1)}, bf16[64,4096]{1,0:T(8,128)(2,1)}, bf16[64,4096]{1,0:T(8,128)(2,1)}, bf16[64,4096]{1,0:T(8,128)(2,1)}) custom-call(bf16[64,4096]{1,0:T(8,128)(2,1)S(1)} %get-tuple-element.8.refs_0_, bf16[64,4096]{1,0:T(8,128)(2,1)S(1)} %get-tuple-element.9.refs_1_, bf16[64,4096]{1,0:T(8,128)(2,1)S(1)} %get-tuple-element.10.refs_2_, ...), custom_call_target="tpu_custom_call" | custom-call | tf_op jit(solution)/shard_map/put_out/pallas_call | solution.py:649
